TPU v7x, 32 devices: a whole 2x2x4 slice. The times are simulated.
32 devices in a mesh: dp: 2 (over x), tp: 16 (over z, y, core).
Axes of the slice: x: 2, y: 2, z: 4, core: 2. Of those that a mesh axis runs over, the one named last changes fastest.
Arguments:
- x_steps: bfloat16 [16, 128, 4096], P(None, 'dp'), parts along dimension 1
- cur_len: int32 [128], P('dp'), parts along dimension 0
- k_cache: bfloat16 [2, 128, 64, 16, 256], P(None, 'dp', None, 'tp'), parts along dimension 1
- v_cache: bfloat16 [2, 128, 64, 16, 256], P(None, 'dp', None, 'tp'), parts along dimension 1
- ln_gain: bfloat16 [2, 4096], replicated
- ln_bias: bfloat16 [2, 4096], replicated
- w_q: bfloat16 [2, 4096, 4096], P(None, None, 'tp')
- w_k: bfloat16 [2, 4096, 4096], P(None, None, 'tp')
- w_v: bfloat16 [2, 4096, 4096], P(None, None, 'tp')
- w_o: bfloat16 [2, 4096, 4096], P(None, 'tp')
- w_in: bfloat16 [2, 4096, 16384], P(None, None, 'tp')
- b_in: bfloat16 [2, 16384], P(None, 'tp')
- w_out: bfloat16 [2, 16384, 4096], P(None, 'tp')
- b_out: bfloat16 [2, 4096], replicated
Outputs:
- output 1: bfloat16 [16, 128, 4096], P(None, 'dp'), parts along dimension 1
- output 2: bfloat16 [2, 128, 64, 16, 256], P(None, 'dp', None, 'tp'), parts along dimension 1
- output 3: bfloat16 [2, 128, 64, 16, 256], P(None, 'dp', None, 'tp'), parts along dimension 1
There are 2 independent parts. A program takes and returns all parts, laid end to end along the dimension named above; an argument that names none is the same for every part.
All inputs are finite; a program needn't handle non-finite values.
Results may differ from a plain program's by a relative error of at most 0.0176966.
Values are sent between devices in bfloat16 or wider.
A program may use at most 1 GiB of HBM per device.

v0:
```python
import jax
import jax.numpy as jnp
from jax import lax
from jax.sharding import PartitionSpec as P

ROT_DIM = 64
LN_EPS = 1e-5


def layer_norm(hidden, gain, bias):
    hid_f32 = hidden.astype(jnp.float32)
    row_mean = jnp.mean(hid_f32, axis=-1, keepdims=True)
    centered = hid_f32 - row_mean
    row_var = jnp.mean(centered * centered, axis=-1, keepdims=True)
    normed = centered * lax.rsqrt(row_var + LN_EPS)
    return (normed * gain.astype(jnp.float32) + bias.astype(jnp.float32)).astype(jnp.bfloat16)


def rotary_tables(positions):
    inv_freq = 1.0 / (10000.0 ** (jnp.arange(0, ROT_DIM, 2).astype(jnp.float32) / ROT_DIM))
    angles = positions.astype(jnp.float32)[:, None] * inv_freq[None, :]
    return jnp.cos(angles)[:, None, :], jnp.sin(angles)[:, None, :]


def apply_rotary(vectors, cos_tab, sin_tab):
    lead_shape = vectors.shape[:-1]
    pairs = vectors[..., :ROT_DIM].reshape(lead_shape + (ROT_DIM // 2, 2))
    even_part = pairs[..., 0]
    odd_part = pairs[..., 1]
    rotated = jnp.stack([even_part * cos_tab - odd_part * sin_tab, odd_part * cos_tab + even_part * sin_tab], axis=-1)
    return jnp.concatenate([rotated.reshape(lead_shape + (ROT_DIM,)), vectors[..., ROT_DIM:]], axis=-1)


def attend(query, k_layer, v_layer, visible):
    score_scale = k_layer.shape[-1] ** -0.5
    scores = jnp.einsum("bhe,bshe->bhs", query, k_layer, preferred_element_type=jnp.float32) * score_scale
    scores = jnp.where(visible, scores, -jnp.inf)
    exp_scores = jnp.exp(scores - jnp.max(scores, axis=-1, keepdims=True))
    attn_probs = (exp_scores / jnp.sum(exp_scores, axis=-1, keepdims=True)).astype(jnp.bfloat16)
    context = jnp.einsum("bhs,bshe->bhe", attn_probs, v_layer, preferred_element_type=jnp.float32)
    return context.astype(jnp.bfloat16)


def step_setup(cur_len, step_idx, cache_len):
    new_pos = cur_len + step_idx
    slot_ids = jnp.arange(cache_len)
    visible = (slot_ids[None, :] <= new_pos[:, None])[:, None, :]
    return new_pos, rotary_tables(new_pos), visible


def layer_update(normed, new_pos, rotary, visible, caches, layer_idx, weights):
    cos_tab, sin_tab = rotary
    k_cache, v_cache = caches
    q_weight, k_weight, v_weight, o_weight, in_weight, in_bias, out_weight = weights
    batch = normed.shape[0]
    n_heads = k_cache.shape[3]
    head_dim = k_cache.shape[4]
    head_shape = (batch, n_heads, head_dim)
    query = jnp.dot(normed, q_weight, preferred_element_type=jnp.float32).reshape(head_shape)
    key_new = jnp.dot(normed, k_weight, preferred_element_type=jnp.float32).reshape(head_shape)
    value_new = jnp.dot(normed, v_weight, preferred_element_type=jnp.float32).astype(jnp.bfloat16).reshape(head_shape)
    query = apply_rotary(query, cos_tab, sin_tab).astype(jnp.bfloat16)
    key_new = apply_rotary(key_new, cos_tab, sin_tab).astype(jnp.bfloat16)
    batch_rows = jnp.arange(batch)
    k_cache = k_cache.at[layer_idx, batch_rows, new_pos].set(key_new)
    v_cache = v_cache.at[layer_idx, batch_rows, new_pos].set(value_new)
    context = attend(query, k_cache[layer_idx], v_cache[layer_idx], visible).reshape(batch, n_heads * head_dim)
    pre_act = jnp.dot(normed, in_weight, preferred_element_type=jnp.float32) + in_bias.astype(jnp.float32)
    gelu_act = jax.nn.gelu(pre_act, approximate=True).astype(jnp.bfloat16)
    layer_part = jnp.dot(context, o_weight, preferred_element_type=jnp.float32) + jnp.dot(gelu_act, out_weight, preferred_element_type=jnp.float32)
    return layer_part, k_cache, v_cache


def decode_shard(x_steps, cur_len, k_cache, v_cache, ln_gain, ln_bias, w_q, w_k, w_v, w_o, w_in, b_in, w_out, b_out):
    n_layers = k_cache.shape[0]
    outputs = []
    for step_idx in range(x_steps.shape[0]):
        new_pos, rotary, visible = step_setup(cur_len, step_idx, k_cache.shape[2])
        hidden = x_steps[step_idx]
        for layer_idx in range(n_layers):
            normed = layer_norm(hidden, ln_gain[layer_idx], ln_bias[layer_idx])
            weights = (w_q[layer_idx], w_k[layer_idx], w_v[layer_idx], w_o[layer_idx], w_in[layer_idx], b_in[layer_idx], w_out[layer_idx])
            layer_part, k_cache, v_cache = layer_update(normed, new_pos, rotary, visible, (k_cache, v_cache), layer_idx, weights)
            layer_sum = lax.psum(layer_part.astype(jnp.bfloat16), "tp")
            hidden = (hidden.astype(jnp.float32) + layer_sum.astype(jnp.float32) + b_out[layer_idx].astype(jnp.float32)).astype(jnp.bfloat16)
        outputs.append(hidden)
    return jnp.stack(outputs), k_cache, v_cache


def solution(mesh):
    cache_spec = P(None, "dp", None, "tp", None)
    in_specs = (P(None, "dp", None), P("dp"), cache_spec, cache_spec, P(None, None), P(None, None),
                P(None, None, "tp"), P(None, None, "tp"), P(None, None, "tp"), P(None, "tp", None),
                P(None, None, "tp"), P(None, "tp"), P(None, "tp", None), P(None, None))
    out_specs = (P(None, "dp", None), cache_spec, cache_spec)
    return jax.shard_map(decode_shard, mesh=mesh, in_specs=in_specs, out_specs=out_specs, check_vma=False)
```

profile of v0, /device:TPU:0, one launch (start us, length us, event | category | flops | bytes accessed | tf_op | source)
XLA Modules:
  0.0 2819.2 jit_solution(1568290066094485674)
XLA Ops:
  145.5 10.0 fusion.64
  155.5 10.1 fusion.66
  165.6 10.0 fusion.68
  175.6 10.0 fusion.70
  185.6 10.2 fusion.72
  195.8 10.1 fusion.74
  205.8 10.0 fusion.76
  215.9 10.0 fusion.78
  244.1 10.1 fusion.84
  254.3 10.0 fusion.86
  264.3 10.0 fusion.88
  274.3 10.0 fusion.90
  284.6 10.5 fusion.92
  381.1 81.7 %all-reduce.21.cloned.1.call-done = bf16[64,4096]{1,0:T(8,128)(2,1)} async-done(((bf16[64,4096]{1,0:T(8,128)(2,1)}), bf16[64,4096]{1,0:T(8,128)(2,1)}) %all-reduce.21.cloned.1.call-update) | async-done | bytes 524304 | tf_op jit(solution)/shard_map/psum | solution.py:84
  468.7 9.9 fusion.28
  530.6 86.3 %all-reduce.23.cloned.1.call-done = bf16[64,4096]{1,0:T(8,128)(2,1)} async-done(((bf16[64,4096]{1,0:T(8,128)(2,1)}), bf16[64,4096]{1,0:T(8,128)(2,1)}) %all-reduce.23.cloned.1.call-update) | async-done | bytes 524304 | tf_op jit(solution)/shard_map/psum | solution.py:84
  681.9 87.8 %all-reduce.25.cloned.1.call-done = bf16[64,4096]{1,0:T(8,128)(2,1)} async-done(((bf16[64,4096]{1,0:T(8,128)(2,1)}), bf16[64,4096]{1,0:T(8,128)(2,1)}) %all-reduce.25.cloned.1.call-update) | async-done | bytes 524304 | tf_op jit(solution)/shard_map/psum | solution.py:84
  775.6 9.9 fusion.24
  836.7 86.3 %all-reduce.27.cloned.1.call-done = bf16[64,4096]{1,0:T(8,128)(2,1)} async-done(((bf16[64,4096]{1,0:T(8,128)(2,1)}), bf16[64,4096]{1,0:T(8,128)(2,1)}) %all-reduce.27.cloned.1.call-update) | async-done | bytes 524304 | tf_op jit(solution)/shard_map/psum | solution.py:84
  928.9 9.9 fusion.22
  989.0 87.6 %all-reduce.29.cloned.1.call-done = bf16[64,4096]{1,0:T(8,128)(2,1)} async-done(((bf16[64,4096]{1,0:T(8,128)(2,1)}), bf16[64,4096]{1,0:T(8,128)(2,1)}) %all-reduce.29.cloned.1.call-update) | async-done | bytes 524304 | tf_op jit(solution)/shard_map/psum | solution.py:84
  1141.3 87.8 %all-reduce.31.cloned.1.call-done = bf16[64,4096]{1,0:T(8,128)(2,1)} async-done(((bf16[64,4096]{1,0:T(8,128)(2,1)}), bf16[64,4096]{1,0:T(8,128)(2,1)}) %all-reduce.31.cloned.1.call-update) | async-done | bytes 524304 | tf_op jit(solution)/shard_map/psum | solution.py:84
  1292.3 88.1 %all-reduce.33.cloned.1.call-done = bf16[64,4096]{1,0:T(8,128)(2,1)} async-done(((bf16[64,4096]{1,0:T(8,128)(2,1)}), bf16[64,4096]{1,0:T(8,128)(2,1)}) %all-reduce.33.cloned.1.call-update) | async-done | bytes 524304 | tf_op jit(solution)/shard_map/psum | solution.py:84
  1444.8 87.9 %all-reduce.35.cloned.1.call-done = bf16[64,4096]{1,0:T(8,128)(2,1)} async-done(((bf16[64,4096]{1,0:T(8,128)(2,1)}), bf16[64,4096]{1,0:T(8,128)(2,1)}) %all-reduce.35.cloned.1.call-update) | async-done | bytes 524304 | tf_op jit(solution)/shard_map/psum | solution.py:84
  1597.3 87.7 %all-reduce.37.cloned.1.call-done = bf16[64,4096]{1,0:T(8,128)(2,1)} async-done(((bf16[64,4096]{1,0:T(8,128)(2,1)}), bf16[64,4096]{1,0:T(8,128)(2,1)}) %all-reduce.37.cloned.1.call-update) | async-done | bytes 524304 | tf_op jit(solution)/shard_map/psum | solution.py:84
  1748.3 88.1 %all-reduce.39.cloned.1.call-done = bf16[64,4096]{1,0:T(8,128)(2,1)} async-done(((bf16[64,4096]{1,0:T(8,128)(2,1)}), bf16[64,4096]{1,0:T(8,128)(2,1)}) %all-reduce.39.cloned.1.call-update) | async-done | bytes 524304 | tf_op jit(solution)/shard_map/psum | solution.py:84
  1899.6 88.1 %all-reduce.41.cloned.1.call-done = bf16[64,4096]{1,0:T(8,128)(2,1)} async-done(((bf16[64,4096]{1,0:T(8,128)(2,1)}), bf16[64,4096]{1,0:T(8,128)(2,1)}) %all-reduce.41.cloned.1.call-update) | async-done | bytes 524304 | tf_op jit(solution)/shard_map/psum | solution.py:84
  2051.1 88.1 %all-reduce.43.cloned.1.call-done = bf16[64,4096]{1,0:T(8,128)(2,1)} async-done(((bf16[64,4096]{1,0:T(8,128)(2,1)}), bf16[64,4096]{1,0:T(8,128)(2,1)}) %all-reduce.43.cloned.1.call-update) | async-done | bytes 524304 | tf_op jit(solution)/shard_map/psum | solution.py:84
  2202.5 88.1 %all-reduce.45.cloned.1.call-done = bf16[64,4096]{1,0:T(8,128)(2,1)} async-done(((bf16[64,4096]{1,0:T(8,128)(2,1)}), bf16[64,4096]{1,0:T(8,128)(2,1)}) %all-reduce.45.cloned.1.call-update) | async-done | bytes 524304 | tf_op jit(solution)/shard_map/psum | solution.py:84
  2354.0 88.1 %all-reduce.47.cloned.1.call-done = bf16[64,4096]{1,0:T(8,128)(2,1)} async-done(((bf16[64,4096]{1,0:T(8,128)(2,1)}), bf16[64,4096]{1,0:T(8,128)(2,1)}) %all-reduce.47.cloned.1.call-update) | async-done | bytes 524304 | tf_op jit(solution)/shard_map/psum | solution.py:84
  2505.5 88.1 %all-reduce.49.cloned.1.call-done = bf16[64,4096]{1,0:T(8,128)(2,1)} async-done(((bf16[64,4096]{1,0:T(8,128)(2,1)}), bf16[64,4096]{1,0:T(8,128)(2,1)}) %all-reduce.49.cloned.1.call-update) | async-done | bytes 524304 | tf_op jit(solution)/shard_map/psum | solution.py:84
  2631.6 169.7 %all-reduce.51.cloned.1.call-done = (bf16[64,4096]{1,0:T(8,128)(2,1)}, bf16[64,4096]{1,0:T(8,128)(2,1)}, bf16[64,4096]{1,0:T(8,128)(2,1)}, bf16[64,4096]{1,0:T(8...) async-done(((bf16[64,4096]{1,0:T(8,128)(2,1)}, ...) | async-done | bytes 8388624 | tf_op jit(solution)/shard_map/psum | solution.py:84
  (1646 shorter events, 1157.8 us)
Async XLA Ops:
  7.2 308.5 %all-reduce.19.cloned.1.call-start = ((), (), s32[]{:S(2)}) async-start(), calls=%async_computation | async-start | bytes 1048576 | tf_op jit(solution)/shard_map/psum | solution.py:84
  18.8 265.5 %copy-start.229 = (f32[64]{0:T(128)}, f32[64]{0:T(128)S(1)}, u32[]{:S(2)}) copy-start(f32[64]{0:T(128)S(1)} %get-tuple-element.544) | copy-start | bytes 772
  20.6 263.7 %copy-start.202 = (f32[1,4096]{1,0:T(1,128)}, f32[1,4096]{1,0:T(1,128)S(1)}, u32[]{:S(2)}) copy-start(f32[1,4096]{1,0:T(1,128)S(1)} %get-tuple-element.342) | copy-start | bytes 49156
  21.2 263.1 %copy-start.204 = (f32[1,4096]{1,0:T(1,128)}, f32[1,4096]{1,0:T(1,128)S(1)}, u32[]{:S(2)}) copy-start(f32[1,4096]{1,0:T(1,128)S(1)} %get-tuple-element.344) | copy-start | bytes 49156
  62.2 400.6 %all-reduce.21.cloned.1.call-start = ((), (), s32[]{:S(2)}) async-start(), calls=%async_computation.1 | async-start | bytes 1048576 | tf_op jit(solution)/shard_map/psum | solution.py:84
  317.3 50.7 %copy-start.33 = (bf16[64,4096]{1,0:T(8,128)(2,1)}, bf16[64,4096]{1,0:T(8,128)(2,1)S(1)}, u32[]{:S(2)}) copy-start(bf16[64,4096]{1,0:T(8,128)(2,1)S(1)} %get-tuple-element.82) | copy-start | bytes 1572868
  368.0 248.9 %all-reduce.23.cloned.1.call-start = ((), (), s32[]{:S(2)}) async-start(), calls=%async_computation.2 | async-start | bytes 1048576 | tf_op jit(solution)/shard_map/psum | solution.py:84
  525.8 93.1 %copy-start.196 = (f32[1,4096]{1,0:T(1,128)S(1)}, f32[1,4096]{1,0:T(1,128)}, u32[]{:S(2)}) copy-start(f32[1,4096]{1,0:T(1,128)} %get-tuple-element.341) | copy-start | bytes 49156
  525.8 93.1 %copy-start.200 = (f32[1,4096]{1,0:T(1,128)S(1)}, f32[1,4096]{1,0:T(1,128)}, u32[]{:S(2)}) copy-start(f32[1,4096]{1,0:T(1,128)} %get-tuple-element.343) | copy-start | bytes 49156
  525.8 243.8 %all-reduce.25.cloned.1.call-start = ((), (), s32[]{:S(2)}) async-start(), calls=%async_computation.3 | async-start | bytes 1048576 | tf_op jit(solution)/shard_map/psum | solution.py:84
  678.6 244.4 %all-reduce.27.cloned.1.call-start = ((), (), s32[]{:S(2)}) async-start(), calls=%async_computation.4 | async-start | bytes 1048576 | tf_op jit(solution)/shard_map/psum | solution.py:84
  832.0 244.6 %all-reduce.29.cloned.1.call-start = ((), (), s32[]{:S(2)}) async-start(), calls=%async_computation.5 | async-start | bytes 1048576 | tf_op jit(solution)/shard_map/psum | solution.py:84
  982.4 96.2 %copy-start.197 = (f32[1,4096]{1,0:T(1,128)S(1)}, f32[1,4096]{1,0:T(1,128)}, u32[]{:S(2)}) copy-start(f32[1,4096]{1,0:T(1,128)} %get-tuple-element.341) | copy-start | bytes 49156
  982.4 96.3 %copy-start.201 = (f32[1,4096]{1,0:T(1,128)S(1)}, f32[1,4096]{1,0:T(1,128)}, u32[]{:S(2)}) copy-start(f32[1,4096]{1,0:T(1,128)} %get-tuple-element.343) | copy-start | bytes 49156
  985.6 243.6 %all-reduce.31.cloned.1.call-start = ((), (), s32[]{:S(2)}) async-start(), calls=%async_computation.6 | async-start | bytes 1048576 | tf_op jit(solution)/shard_map/psum | solution.py:84
  1138.1 242.3 %all-reduce.33.cloned.1.call-start = ((), (), s32[]{:S(2)}) async-start(), calls=%async_computation.7 | async-start | bytes 1048576 | tf_op jit(solution)/shard_map/psum | solution.py:84
  1289.4 243.3 %all-reduce.35.cloned.1.call-start = ((), (), s32[]{:S(2)}) async-start(), calls=%async_computation.8 | async-start | bytes 1048576 | tf_op jit(solution)/shard_map/psum | solution.py:84
  1441.7 243.3 %all-reduce.37.cloned.1.call-start = ((), (), s32[]{:S(2)}) async-start(), calls=%async_computation.9 | async-start | bytes 1048576 | tf_op jit(solution)/shard_map/psum | solution.py:84
  1594.0 242.4 %all-reduce.39.cloned.1.call-start = ((), (), s32[]{:S(2)}) async-start(), calls=%async_computation.10 | async-start | bytes 1048576 | tf_op jit(solution)/shard_map/psum | solution.py:84
  1745.3 242.4 %all-reduce.41.cloned.1.call-start = ((), (), s32[]{:S(2)}) async-start(), calls=%async_computation.11 | async-start | bytes 1048576 | tf_op jit(solution)/shard_map/psum | solution.py:84
  1896.7 242.6 %all-reduce.43.cloned.1.call-start = ((), (), s32[]{:S(2)}) async-start(), calls=%async_computation.12 | async-start | bytes 1048576 | tf_op jit(solution)/shard_map/psum | solution.py:84
  2048.2 242.4 %all-reduce.45.cloned.1.call-start = ((), (), s32[]{:S(2)}) async-start(), calls=%async_computation.13 | async-start | bytes 1048576 | tf_op jit(solution)/shard_map/psum | solution.py:84
  2199.6 242.5 %all-reduce.47.cloned.1.call-start = ((), (), s32[]{:S(2)}) async-start(), calls=%async_computation.14 | async-start | bytes 1048576 | tf_op jit(solution)/shard_map/psum | solution.py:84
  2351.0 242.6 %all-reduce.49.cloned.1.call-start = ((), (), s32[]{:S(2)}) async-start(), calls=%async_computation.15 | async-start | bytes 1048576 | tf_op jit(solution)/shard_map/psum | solution.py:84
  2502.6 298.8 %all-reduce.51.cloned.1.call-start = ((), (), s32[]{:S(2)}) async-start(), calls=%async_computation.16 | async-start | bytes 16777216 | tf_op jit(solution)/shard_map/psum | solution.py:84
  2631.6 169.8 %copy-start.32 = (f32[1,4096]{1,0:T(1,128)S(1)}, f32[1,4096]{1,0:T(1,128)}, u32[]{:S(2)}) copy-start(f32[1,4096]{1,0:T(1,128)} %get-tuple-element.339) | copy-start | bytes 49156
  2631.6 169.8 %copy-start.34 = (bf16[64,4096]{1,0:T(8,128)(2,1)S(1)}, bf16[64,4096]{1,0:T(8,128)(2,1)}, u32[]{:S(2)}) copy-start(bf16[64,4096]{1,0:T(8,128)(2,1)} %copy-done.33) | copy-start | bytes 1572868
  2631.6 171.2 %copy-start.36 = (bf16[64,4096]{1,0:T(8,128)(2,1)S(1)}, bf16[64,4096]{1,0:T(8,128)(2,1)}, u32[]{:S(2)}) copy-start(bf16[64,4096]{1,0:T(8,128)(2,1)} %copy-done.35) | copy-start | bytes 1572868
  2631.6 172.5 %copy-start.38 = (bf16[64,4096]{1,0:T(8,128)(2,1)S(1)}, bf16[64,4096]{1,0:T(8,128)(2,1)}, u32[]{:S(2)}) copy-start(bf16[64,4096]{1,0:T(8,128)(2,1)} %copy-done.37) | copy-start | bytes 1572868
  2631.6 173.8 %copy-start.40 = (bf16[64,4096]{1,0:T(8,128)(2,1)S(1)}, bf16[64,4096]{1,0:T(8,128)(2,1)}, u32[]{:S(2)}) copy-start(bf16[64,4096]{1,0:T(8,128)(2,1)} %copy-done.39) | copy-start | bytes 1572868
  2631.6 174.0 %copy-start.42 = (bf16[64,4096]{1,0:T(8,128)(2,1)S(1)}, bf16[64,4096]{1,0:T(8,128)(2,1)}, u32[]{:S(2)}) copy-start(bf16[64,4096]{1,0:T(8,128)(2,1)} %copy-done.41) | copy-start | bytes 1572868
  2631.6 174.2 %copy-start.44 = (bf16[64,4096]{1,0:T(8,128)(2,1)S(1)}, bf16[64,4096]{1,0:T(8,128)(2,1)}, u32[]{:S(2)}) copy-start(bf16[64,4096]{1,0:T(8,128)(2,1)} %copy-done.43) | copy-start | bytes 1572868
  (296 other events, 3466.0 us)
Sparse Core Ops, SparseCore 0:
  62.3 94.8 all-reduce.18
  368.1 94.6 all-reduce.20
  526.0 90.8 all-reduce.22
  678.8 90.8 all-reduce.24
  832.1 90.8 all-reduce.26
  985.7 90.8 all-reduce.28
  1138.2 90.8 all-reduce.30
  1289.5 90.8 all-reduce.32
  1441.8 90.8 all-reduce.34
  1594.1 90.8 all-reduce.36
  1745.4 90.9 all-reduce.38
  1896.8 90.8 all-reduce.40
  2048.3 90.8 all-reduce.42
  2199.7 90.9 all-reduce.44
  2351.1 90.8 all-reduce.46
  2502.7 90.8 all-reduce.48
  2631.7 169.6 all-reduce.50
where the time goes:
time: 2840 us; the launch traced here: 2820 us
  waiting for transfers between devices  1480 us (52%)
  matrix products  665 us (23%)
  local copies, waits for them, and re-layouts  568 us (20%)
  other arithmetic  84.7 us (3%)
    psum x17, waiting for transfers between devices, decode_shard(): layer_sum = lax.psum(layer_part.astype(jnp.bfloat16), 'tp')  1480 us
    dot_general x32, matrix products, layer_update(): jnp.dot(gelu_act, out_weight, preferred_element_type=jnp.float32)  307 us
    scatter x32, local copies, waits for them, and re-layouts, layer_update(): v_cache = v_cache.at[layer_idx, batch_rows, new_pos].set(value_new)  261 us
    scatter x32, local copies, waits for them, and re-layouts, layer_update(): k_cache = k_cache.at[layer_idx, batch_rows, new_pos].set(key_new)  257 us
    dot_general x32, matrix products, layer_update(): jnp.dot(context, o_weight, preferred_element_type=jnp.float32)  94.2 us
    dot_general x32, matrix products, layer_update(): jnp.dot(normed, v_weight, preferred_element_type=jnp.float32)  78.6 us
    dot_general x32, matrix products, attend(): jnp.einsum('bhe,bshe->bhs', query, k_layer, preferred_element_type=jnp.fl...  71.5 us
    dot_general x32, matrix products, attend(): jnp.einsum('bhs,bshe->bhe', attn_probs, v_layer, preferred_element_type=j...  63.1 us
  transfers between devices with their start and end apart: 17, of which 16 were waited for; matrix products, arithmetic and copies ran while one was open for 11% of the time, Pallas kernels for 0%

commit v1 on v0

v1 whole, which is shorter than its diff:
```python
import jax
import jax.numpy as jnp
from jax import lax
from jax.sharding import PartitionSpec as P

ROT_DIM = 64
LN_EPS = 1e-5
TP = 16
CHUNKS = 2


def layer_norm(hidden, gain, bias):
    hid_f32 = hidden.astype(jnp.float32)
    row_mean = jnp.mean(hid_f32, axis=-1, keepdims=True)
    centered = hid_f32 - row_mean
    row_var = jnp.mean(centered * centered, axis=-1, keepdims=True)
    normed = centered * lax.rsqrt(row_var + LN_EPS)
    return (normed * gain.astype(jnp.float32) + bias.astype(jnp.float32)).astype(jnp.bfloat16)


def rotary_full(positions, width):
    inv_freq = 1.0 / (10000.0 ** (jnp.arange(0, ROT_DIM, 2).astype(jnp.float32) / ROT_DIM))
    angles = positions.astype(jnp.float32)[:, None] * inv_freq[None, :]
    cos = jnp.repeat(jnp.cos(angles), 2, axis=1)
    sin = jnp.repeat(jnp.sin(angles), 2, axis=1) * jnp.where(jnp.arange(ROT_DIM) % 2 == 0, -1.0, 1.0)
    rest = width - ROT_DIM
    return jnp.pad(cos, ((0, 0), (0, rest)), constant_values=1.0), jnp.pad(sin, ((0, 0), (0, rest)))


def rotate(vec, cos, sin):
    even = jnp.arange(vec.shape[1]) % 2 == 0
    swapped = jnp.where(even, jnp.roll(vec, -1, axis=1), jnp.roll(vec, 1, axis=1))
    return vec * cos + swapped * sin


def write_slots(cache, new, first):
    steps = jnp.arange(new.shape[0])
    offset = jnp.arange(cache.shape[1])[None, :] - first[:, None]
    one_hot = (offset[:, :, None] == steps).astype(jnp.bfloat16)
    placed = jnp.einsum("bst,tbe->bse", one_hot, new, preferred_element_type=jnp.float32).astype(jnp.bfloat16)
    written = (offset >= 0) & (offset < new.shape[0])
    return jnp.where(written[:, :, None], placed, cache)


def layer_update(normed, cos, sin, cur_len, first_step, k_cache, v_cache, weights):
    w_q, w_k, w_v, w_o, w_in, b_in, w_out = weights
    batch, slots, dim = k_cache.shape
    steps = normed.shape[0] // batch
    query = rotate(jnp.dot(normed, w_q, preferred_element_type=jnp.float32), cos, sin).astype(jnp.bfloat16)
    key = rotate(jnp.dot(normed, w_k, preferred_element_type=jnp.float32), cos, sin).astype(jnp.bfloat16)
    value = jnp.dot(normed, w_v, preferred_element_type=jnp.float32).astype(jnp.bfloat16)
    first = cur_len + first_step
    k_cache = write_slots(k_cache, key.reshape(steps, batch, dim), first)
    v_cache = write_slots(v_cache, value.reshape(steps, batch, dim), first)
    scores = jnp.einsum("tbe,bse->bts", query.reshape(steps, batch, dim), k_cache, preferred_element_type=jnp.float32) * (dim ** -0.5)
    visible = jnp.arange(slots) <= (first[:, None] + jnp.arange(steps))[:, :, None]
    scores = jnp.where(visible, scores, -jnp.inf)
    exp_scores = jnp.exp(scores - jnp.max(scores, axis=-1, keepdims=True))
    probs = (exp_scores / jnp.sum(exp_scores, axis=-1, keepdims=True)).astype(jnp.bfloat16)
    context = jnp.einsum("bts,bse->tbe", probs, v_cache, preferred_element_type=jnp.float32)
    context = context.astype(jnp.bfloat16).reshape(steps * batch, dim)
    pre_act = jnp.dot(normed, w_in, preferred_element_type=jnp.float32) + b_in.astype(jnp.float32)
    act = jax.nn.gelu(pre_act, approximate=True).astype(jnp.bfloat16)
    part = jnp.dot(context, w_o, preferred_element_type=jnp.float32) + jnp.dot(act, w_out, preferred_element_type=jnp.float32)
    return part.astype(jnp.bfloat16), k_cache, v_cache


def decode_shard(x_steps, cur_len, k_cache, v_cache, ln_gain, ln_bias, w_q, w_k, w_v, w_o, w_in, b_in, w_out, b_out):
    n_layers, batch, slots, _, dim = k_cache.shape
    total, _, width = x_steps.shape
    steps = total // CHUNKS
    rows = steps * batch
    own = rows // TP
    me = lax.axis_index("tp")
    k_caches = [k_cache[layer, :, :, 0] for layer in range(n_layers)]
    v_caches = [v_cache[layer, :, :, 0] for layer in range(n_layers)]
    xs = [x_steps[c * steps:(c + 1) * steps].reshape(rows, width) for c in range(CHUNKS)]
    normed = [layer_norm(x, ln_gain[0], ln_bias[0]) for x in xs]
    hidden = [lax.dynamic_slice_in_dim(x, me * own, own) for x in xs]
    tables = []
    for c in range(CHUNKS):
        pos = (cur_len[None, :] + (c * steps + jnp.arange(steps))[:, None]).reshape(rows)
        tables.append(rotary_full(pos, dim))
    outputs = []
    for layer in range(n_layers):
        weights = (w_q[layer], w_k[layer], w_v[layer], w_o[layer], w_in[layer], b_in[layer], w_out[layer])
        for c in range(CHUNKS):
            cos, sin = tables[c]
            part, k_caches[layer], v_caches[layer] = layer_update(
                normed[c], cos, sin, cur_len, c * steps, k_caches[layer], v_caches[layer], weights)
            mine = lax.psum_scatter(part, "tp", scatter_dimension=0, tiled=True)
            hidden[c] = (hidden[c].astype(jnp.float32) + mine.astype(jnp.float32) + b_out[layer].astype(jnp.float32)).astype(jnp.bfloat16)
            if layer + 1 < n_layers:
                send = layer_norm(hidden[c], ln_gain[layer + 1], ln_bias[layer + 1])
                normed[c] = lax.all_gather(send, "tp", axis=0, tiled=True)
            else:
                outputs.append(lax.all_gather(hidden[c], "tp", axis=0, tiled=True).reshape(steps, batch, width))
    return jnp.concatenate(outputs), jnp.stack(k_caches)[:, :, :, None], jnp.stack(v_caches)[:, :, :, None]


def solution(mesh):
    cache_spec = P(None, "dp", None, "tp", None)
    in_specs = (P(None, "dp", None), P("dp"), cache_spec, cache_spec, P(None, None), P(None, None),
                P(None, None, "tp"), P(None, None, "tp"), P(None, None, "tp"), P(None, "tp", None),
                P(None, None, "tp"), P(None, "tp"), P(None, "tp", None), P(None, None))
    out_specs = (P(None, "dp", None), cache_spec, cache_spec)
    return jax.shard_map(decode_shard, mesh=mesh, in_specs=in_specs, out_specs=out_specs, check_vma=False)
```

time: 2840 us -> 619 us (0.22)
  waiting for transfers between devices: 1480 us -> 348 us
  local copies, waits for them, and re-layouts: 568 us -> 28.8 us
  matrix products: 665 us -> 172 us
  other arithmetic: 84.7 us -> 45.5 us
    psum x17 -> x0, waiting for transfers between devices: 1480 us -> none  [decode_shard(): layer_sum = lax.psum(layer_part.astype(jnp.bfloat16), 'tp')]
    scatter x64 -> x0, local copies, waits for them, and re-layouts: 519 us -> none  [the longest x32 261 us: layer_update(): v_cache = v_cache.at[layer_idx, batch_rows, new_pos].set(value_new)]
    dot_general x224 -> x36, matrix products: 665 us -> 172 us  [the longest x4 78.5 us: layer_update(): jnp.dot(act, w_out, preferred_element_type=jnp.float32)]
    reduce_scatter x0 -> x4, waiting for transfers between devices: none -> 202 us  [decode_shard(): mine = lax.psum_scatter(part, 'tp', scatter_dimension=0, tiled=True)]
    all_gather x0 -> x4, waiting for transfers between devices: none -> 145 us  [the longest x2 94.5 us: decode_shard(): lax.all_gather(hidden[c], 'tp', axis=0, tiled=True)]
  transfers between devices with their start and end apart: 17 -> 8, of which waited for: 16 -> 8; matrix products, arithmetic and copies ran while one was open for 11% -> 25% of each run, Pallas kernels for 0% -> 0%
where the time goes in v1:
time: 619 us; the launch traced here: 610 us
  waiting for transfers between devices  348 us (56%)
  matrix products  172 us (28%)
  other arithmetic  45.5 us (7%)
  local copies, waits for them, and re-layouts  28.8 us (5%)
  between operations  15.5 us (3%)
    reduce_scatter x4, waiting for transfers between devices, decode_shard(): mine = lax.psum_scatter(part, 'tp', scatter_dimension=0, tiled=True)  202 us
    all_gather x2, waiting for transfers between devices, decode_shard(): lax.all_gather(hidden[c], 'tp', axis=0, tiled=True)  94.5 us
    dot_general x4, matrix products, layer_update(): jnp.dot(act, w_out, preferred_element_type=jnp.float32)  78.5 us
    all_gather x2, waiting for transfers between devices, decode_shard(): normed[c] = lax.all_gather(send, 'tp', axis=0, tiled=True)  50.8 us
    dot_general x4, matrix products, layer_update(): jnp.dot(context, w_o, preferred_element_type=jnp.float32)  29.1 us
    dot_general x8, matrix products, write_slots(): jnp.einsum('bst,tbe->bse', one_hot, new, preferred_element_type=jnp.float32)  19.8 us
    dot_general x4, matrix products, layer_update(): jnp.dot(normed, w_v, preferred_element_type=jnp.float32)  15.1 us
    dot_general x4, matrix products, layer_update(): jnp.dot(normed, w_k, preferred_element_type=jnp.float32)  14.2 us
  transfers between devices with their start and end apart: 8, of which 8 were waited for; matrix products, arithmetic and copies ran while one was open for 25% of the time, Pallas kernels for 0%

profile of v1, /device:TPU:0, one launch (start us, length us, event | category | flops | bytes accessed | tf_op | source)
XLA Modules:
  0.0 610.1 jit_solution(15409204793237625259)
XLA Ops:
  11.2 2.8 convert_reduce_fusion.1
  14.1 4.5 fusion.12
  22.4 6.1 fusion.15
  38.0 4.9 fusion.140
  46.3 3.4 fusion.74
  50.7 2.9 fusion.75
  56.2 19.6 %fusion.26 = f32[512,4096]{1,0:T(8,128)} fusion(bf16[2,1024,4096]{2,1,0:T(8,128)(2,1)} %param.26, bf16[512,4096]{1,0:T(8,128)(2,1)} %bitcast.211, bf16[2,4096,1024]{2,1,0:T(8,128)(2,1)} %param.24, f32[1024]{0:T(1024)S(1)} %bitcast.242), kind=kOutput, calls=%fused_computation.31 | convolution fusion | flops 8595177472 | bytes 29364224 | tf_op jit(solution)/shard_map/dot_general | solution.py:64
  75.9 7.3 %add_convert_fusion.3 = bf16[512,4096]{1,0:T(8,128)(2,1)} fusion(f32[512,4096]{1,0:T(8,128)} %fusion.26, bf16[512,256]{1,0:T(8,128)(2,1)S(1)} %bitcast.221, bf16[2,256,4096]{2,1,0:T(8,128)(2,1)} %param.23), kind=kOutput, calls=%fused_computation.40 | convolution fusion | flops 1077936128 | bytes 14942208 | tf_op jit(solution)/shard_map/dot_general | solution.py:64
  83.3 4.3 fusion.92
  99.6 3.0 fusion.143
  105.3 19.6 %fusion.24 = f32[512,4096]{1,0:T(8,128)} fusion(bf16[2,1024,4096]{2,1,0:T(8,128)(2,1)} %param.26, bf16[512,4096]{1,0:T(8,128)(2,1)} %bitcast.205, bf16[2,4096,1024]{2,1,0:T(8,128)(2,1)} %param.24, f32[1024]{0:T(1024)S(1)} %bitcast.243), kind=kOutput, calls=%fused_computation.29 | convolution fusion | flops 8595177472 | bytes 29364224 | tf_op jit(solution)/shard_map/dot_general | solution.py:64
  125.0 7.3 %add_convert_fusion.1 = bf16[512,4096]{1,0:T(8,128)(2,1)} fusion(f32[512,4096]{1,0:T(8,128)} %fusion.24, bf16[512,256]{1,0:T(8,128)(2,1)S(1)} %bitcast.218, bf16[2,256,4096]{2,1,0:T(8,128)(2,1)} %param.23), kind=kOutput, calls=%fused_computation.38 | convolution fusion | flops 1077936128 | bytes 14942208 | tf_op jit(solution)/shard_map/dot_general | solution.py:64
  133.6 6.1 fusion.257
  139.6 19.4 %reduce-scatter.5.cloned.1.call-done = bf16[32,4096]{1,0:T(8,128)(2,1)} async-done(((bf16[512,4096]{1,0:T(8,128)(2,1)}), bf16[32,4096]{1,0:T(8,128)(2,1)}) %reduce-scatter.5.cloned.1.call-update) | async-done | bytes 262160 | tf_op jit(solution)/shard_map/reduce_scatter | solution.py:91
  159.1 75.9 %reduce-scatter.9.cloned.1.call-done = bf16[32,4096]{1,0:T(8,128)(2,1)} async-done(((bf16[512,4096]{1,0:T(8,128)(2,1)}), bf16[32,4096]{1,0:T(8,128)(2,1)}) %reduce-scatter.9.cloned.1.call-update) | async-done | bytes 262160 | tf_op jit(solution)/shard_map/reduce_scatter | solution.py:91
  238.7 49.0 %all-gather.5.cloned.1.call-done = bf16[512,4096]{1,0:T(8,128)(2,1)} async-done(((bf16[32,4096]{1,0:T(8,128)(2,1)}), bf16[512,4096]{1,0:T(8,128)(2,1)}) %all-gather.5.cloned.1.call-update) | async-done | bytes 4194320 | tf_op jit(solution)/shard_map/all_gather | solution.py:95
  287.7 4.3 fusion.80
  297.3 2.9 fusion.72
  301.1 3.6 fusion.146
  304.8 2.8 fusion.73
  310.2 19.6 %fusion.18 = f32[512,4096]{1,0:T(8,128)} fusion(bf16[2,1024,4096]{2,1,0:T(8,128)(2,1)} %param.26, bf16[512,4096]{1,0:T(8,128)(2,1)} %all-gather.5.cloned.1.call-done, bf16[2,4096,1024]{2,1,0:T(8,128)(2,1)} %param.24, f32[1024]{0:T(1024)S(1)} %bitcast.240), kind=kOutput, calls=%fused_computation.23 | convolution fusion | flops 8595177472 | bytes 29364224 | tf_op jit(solution)/shard_map/dot_general | solution.py:64
  329.8 7.3 %add_convert_fusion.2 = bf16[512,4096]{1,0:T(8,128)(2,1)} fusion(f32[512,4096]{1,0:T(8,128)} %fusion.18, bf16[512,256]{1,0:T(8,128)(2,1)S(1)} %bitcast.219, bf16[2,256,4096]{2,1,0:T(8,128)(2,1)} %param.23), kind=kOutput, calls=%fused_computation.39 | convolution fusion | flops 1077936128 | bytes 14942208 | tf_op jit(solution)/shard_map/dot_general | solution.py:64
  339.1 4.3 fusion.78
  351.9 3.6 fusion.149
  358.2 19.6 %fusion.16 = f32[512,4096]{1,0:T(8,128)} fusion(bf16[2,1024,4096]{2,1,0:T(8,128)(2,1)} %param.26, bf16[512,4096]{1,0:T(8,128)(2,1)} %all-gather.9.cloned.1.call-done, bf16[2,4096,1024]{2,1,0:T(8,128)(2,1)} %param.24, f32[1024]{0:T(1024)S(1)} %bitcast.241), kind=kOutput, calls=%fused_computation.21 | convolution fusion | flops 8595177472 | bytes 29364224 | tf_op jit(solution)/shard_map/dot_general | solution.py:64
  377.8 7.3 %add_convert_fusion = bf16[512,4096]{1,0:T(8,128)(2,1)} fusion(f32[512,4096]{1,0:T(8,128)} %fusion.16, bf16[512,256]{1,0:T(8,128)(2,1)S(1)} %bitcast.220, bf16[2,256,4096]{2,1,0:T(8,128)(2,1)} %param.23), kind=kOutput, calls=%fused_computation.37 | convolution fusion | flops 1077936128 | bytes 14942208 | tf_op jit(solution)/shard_map/dot_general | solution.py:64
  385.2 30.1 %reduce-scatter.7.cloned.1.call-done = bf16[32,4096]{1,0:T(8,128)(2,1)} async-done(((bf16[512,4096]{1,0:T(8,128)(2,1)}), bf16[32,4096]{1,0:T(8,128)(2,1)}) %reduce-scatter.7.cloned.1.call-update) | async-done | bytes 262160 | tf_op jit(solution)/shard_map/reduce_scatter | solution.py:91
  415.3 76.3 %reduce-scatter.11.cloned.1.call-done = bf16[32,4096]{1,0:T(8,128)(2,1)} async-done(((bf16[512,4096]{1,0:T(8,128)(2,1)}), bf16[32,4096]{1,0:T(8,128)(2,1)}) %reduce-scatter.11.cloned.1.call-update) | async-done | bytes 262160 | tf_op jit(solution)/shard_map/reduce_scatter | solution.py:91
  494.3 4.1 maximum_bitcast_fusion
  500.8 43.0 %all-gather.7.cloned.1.call-done = bf16[512,4096]{1,0:T(8,128)(2,1)} async-done(((bf16[32,4096]{1,0:T(8,128)(2,1)}), bf16[512,4096]{1,0:T(8,128)(2,1)}) %all-gather.7.cloned.1.call-update) | async-done | bytes 4194320 | tf_op jit(solution)/shard_map/all_gather | solution.py:97
  543.8 51.5 %all-gather.11.cloned.1.call-done = bf16[512,4096]{1,0:T(8,128)(2,1)} async-done(((bf16[32,4096]{1,0:T(8,128)(2,1)}), bf16[512,4096]{1,0:T(8,128)(2,1)}) %all-gather.11.cloned.1.call-update) | async-done | bytes 4194320 | tf_op jit(solution)/shard_map/all_gather | solution.py:97
  595.3 7.6 %pad_maximum_fusion = bf16[16,64,4096]{2,1,0:T(8,128)(2,1)} fusion(bf16[8,64,4096]{2,1,0:T(8,128)(2,1)} %bitcast.217, bf16[8,64,4096]{2,1,0:T(8,128)(2,1)} %bitcast.216), kind=kLoop, calls=%fused_computation.20 | loop fusion | flops 4194304 | bytes 16777216 | tf_op jit(solution)/shard_map/concatenate | solution.py:98
  (230 shorter events, 70.4 us)
Async XLA Ops:
  7.2 151.9 %reduce-scatter.5.cloned.1.call-start = ((), (), s32[]{:S(2)}) async-start(), calls=%async_computation.4 | async-start | bytes 4456448 | tf_op jit(solution)/shard_map/reduce_scatter | solution.py:91
  7.2 84.6 %copy-start.37 = (pred[256]{0:T(512)(128)(4,1)}, pred[256]{0:T(512)(128)(4,1)S(1)}, u32[]{:S(2)}) copy-start(pred[256]{0:T(512)(128)(4,1)S(1)} %fusion.240) | copy-start | bytes 772
  14.1 5.8 copy-start
  22.4 6.1 %copy-start.51 = (bf16[2,4096,256]{2,1,0:T(8,128)(2,1)S(1)}, bf16[2,4096,256]{2,1,0:T(8,128)(2,1)}, u32[]{:S(2)}) copy-start(bf16[2,4096,256]{2,1,0:T(8,128)(2,1)} %param.20) | copy-start | bytes 12582916
  37.1 5.8 copy-start.15
  37.9 5.0 copy-start.41
  38.0 5.0 copy-start.42
  38.0 5.0 copy-start.43
  38.0 5.0 copy-start.44
  44.1 5.7 copy-start.24
  44.1 6.6 %copy-start.18 = (s32[64,64]{1,0:T(8,128)S(1)}, s32[64,64]{1,0:T(8,128)}, u32[]{:S(2)}) copy-start(s32[64,64]{1,0:T(8,128)} %iota_subtract_fusion.1) | copy-start | bytes 49156
  44.1 6.6 %copy-start.28 = (bf16[512,256]{1,0:T(8,128)(2,1)S(1)}, bf16[512,256]{1,0:T(8,128)(2,1)}, u32[]{:S(2)}) copy-start(bf16[512,256]{1,0:T(8,128)(2,1)} %fusion.140) | copy-start | bytes 786436
  50.4 5.8 copy-start.47
  83.2 151.8 %reduce-scatter.9.cloned.1.call-start = ((), (), s32[]{:S(2)}) async-start(), calls=%async_computation.8 | async-start | bytes 4456448 | tf_op jit(solution)/shard_map/reduce_scatter | solution.py:91
  83.2 5.3 copy-start.52
  95.3 7.4 %copy-start.20 = (s32[64,64]{1,0:T(8,128)}, s32[64,64]{1,0:T(8,128)S(1)}, u32[]{:S(2)}) copy-start(s32[64,64]{1,0:T(8,128)S(1)} %iota_subtract_fusion) | copy-start | bytes 49156
  95.4 7.3 %copy-start.26 = (s32[64,8]{1,0:T(8,128)}, s32[64,8]{1,0:T(8,128)S(1)}, u32[]{:S(2)}) copy-start(s32[64,8]{1,0:T(8,128)S(1)} %iota_add_fusion) | copy-start | bytes 6148
  104.3 20.7 %copy-start.6 = (bf16[64,64,256]{2,1,0:T(8,128)(2,1)}, bf16[64,64,256]{2,1,0:T(8,128)(2,1)S(1)}, u32[]{:S(2)}) copy-start(bf16[64,64,256]{2,1,0:T(8,128)(2,1)S(1)} %convert_select_fusion.3) | copy-start | bytes 6291460
  132.2 155.5 %all-gather.5.cloned.1.call-start = ((), (), s32[]{:S(2)}) async-start(), calls=%async_computation.5 | async-start | bytes 4456448 | tf_op jit(solution)/shard_map/all_gather | solution.py:95
  133.6 103.4 %copy-start.30 = (f32[1,4096]{1,0:T(1,128)S(1)}, f32[1,4096]{1,0:T(1,128)}, u32[]{:S(2)}) copy-start(f32[1,4096]{1,0:T(1,128)} %get-tuple-element.67) | copy-start | bytes 49156
  133.6 103.4 %copy-start.31 = (f32[1,4096]{1,0:T(1,128)S(1)}, f32[1,4096]{1,0:T(1,128)}, u32[]{:S(2)}) copy-start(f32[1,4096]{1,0:T(1,128)} %get-tuple-element.69) | copy-start | bytes 49156
  238.1 101.0 %all-gather.9.cloned.1.call-start = ((), (), s32[]{:S(2)}) async-start(), calls=%async_computation.9 | async-start | bytes 4456448 | tf_op jit(solution)/shard_map/all_gather | solution.py:95
  238.7 176.6 %reduce-scatter.7.cloned.1.call-start = ((), (), s32[]{:S(2)}) async-start(), calls=%async_computation.6 | async-start | bytes 4456448 | tf_op jit(solution)/shard_map/reduce_scatter | solution.py:91
  287.7 5.3 copy-start.58
  304.8 5.4 copy-start.45
  337.1 154.4 %reduce-scatter.11.cloned.1.call-start = ((), (), s32[]{:S(2)}) async-start(), calls=%async_computation.10 | async-start | bytes 4456448 | tf_op jit(solution)/shard_map/reduce_scatter | solution.py:91
  339.1 5.3 copy-start.57
  357.1 20.7 %copy-start.8 = (bf16[64,64,256]{2,1,0:T(8,128)(2,1)}, bf16[64,64,256]{2,1,0:T(8,128)(2,1)S(1)}, u32[]{:S(2)}) copy-start(bf16[64,64,256]{2,1,0:T(8,128)(2,1)S(1)} %convert_select_fusion.1) | copy-start | bytes 6291460
  385.1 106.4 %copy-start.32 = (f32[1,4096]{1,0:T(1,128)S(1)}, f32[1,4096]{1,0:T(1,128)}, u32[]{:S(2)}) copy-start(f32[1,4096]{1,0:T(1,128)} %get-tuple-element.63) | copy-start | bytes 49156
  385.1 109.2 %copy-start.2 = (bf16[64,64,256]{2,1,0:T(8,128)(2,1)S(1)}, bf16[64,64,256]{2,1,0:T(8,128)(2,1)}, u32[]{:S(2)}) copy-start(bf16[64,64,256]{2,1,0:T(8,128)(2,1)} %copy-done.1) | copy-start | bytes 6291460
  385.1 158.7 %all-gather.7.cloned.1.call-start = ((), (), s32[]{:S(2)}) async-start(), calls=%async_computation.7 | async-start | bytes 4456448 | tf_op jit(solution)/shard_map/all_gather | solution.py:97
  493.5 101.8 %all-gather.11.cloned.1.call-start = ((), (), s32[]{:S(2)}) async-start(), calls=%async_computation.11 | async-start | bytes 4456448 | tf_op jit(solution)/shard_map/all_gather | solution.py:97
  (35 other events, 111.3 us)
Sparse Core Ops, SparseCore 0:
  83.3 75.7 reduce-scatter.4
  162.9 71.9 reduce-scatter.8
  238.2 49.4 all-gather.4
  289.7 49.3 all-gather.8
  343.4 71.8 reduce-scatter.6
  419.5 71.9 reduce-scatter.10
  494.2 49.5 all-gather.6
  546.0 49.3 all-gather.10

commit v2 on v0

v2 whole, which is shorter than its diff:
```python
import functools

import jax
import jax.numpy as jnp
from jax import lax
from jax.experimental import pallas as pl
from jax.experimental.pallas import tpu as pltpu
from jax.sharding import PartitionSpec as P

ROT_DIM = 64
LN_EPS = 1e-5
TP = 16
CHIPS = 8
STREAMS = 4
BF16 = jnp.bfloat16
F32 = jnp.float32
VMEM_LIMIT = 67_000_000
SLOT = {0: 0, -1: 1, 1: 2, -2: 3, 2: 4, -3: 5, 3: 6, 4: 7, -4: 7}
OFFSETS = (0, -1, 1, -2, 2, -3, 3, 4)


def ring_of_chip(chip):
    z, y = lax.div(chip, 2), lax.rem(chip, 2)
    return z + y * (7 - 2 * z)


def chip_of_ring(pos):
    pos = lax.rem(pos + 2 * CHIPS, CHIPS)
    y = lax.div(pos, 4)
    z = pos + y * (7 - 2 * pos)
    return 2 * z + y


def norm_rows(x, gain, bias):
    mean = jnp.mean(x, axis=-1, keepdims=True)
    centered = x - mean
    var = jnp.mean(centered * centered, axis=-1, keepdims=True)
    return (centered * lax.rsqrt(var + LN_EPS) * gain + bias).astype(BF16)


def rotate(vec, cos, sin):
    head, rest = vec[:, :128], vec[:, 128:]
    even = lax.rem(lax.broadcasted_iota(jnp.int32, head.shape, 1), 2) == 0
    swapped = jnp.where(even, pltpu.roll(head, 127, 1), pltpu.roll(head, 1, 1))
    return jnp.concatenate([head * cos + swapped * sin, rest], axis=1).astype(BF16)


def project(lhs_piece, rows, cos_of, sin_of, w_qkv, w_in, b_in_of, qkv_out, act_out):
    def product(w_ref_cols):
        total = None
        for i in range(STREAMS):
            lhs = lhs_piece(i)
            depth = lhs.shape[1]
            term = jnp.dot(lhs, w_ref_cols(i * depth, depth), preferred_element_type=F32)
            total = term if total is None else total + term
        return total

    def put(ref, index, cols, value):
        at = 0
        for first, count in rows:
            if index is None:
                ref[pl.ds(first, count), cols] = value[at:at + count]
            else:
                ref[index, pl.ds(first, count), cols] = value[at:at + count]
            at += count

    def qk_body(i, carry):
        value = product(lambda k0, depth: w_qkv[i, k0:k0 + depth, :])
        put(qkv_out, i, slice(None), rotate(value, cos_of(), sin_of()))
        return carry

    lax.fori_loop(0, 2, qk_body, 0)
    put(qkv_out, 2, slice(None), product(lambda k0, depth: w_qkv[2, k0:k0 + depth, :]).astype(BF16))
    tile = min(256, w_in.shape[1])

    def in_body(n, carry):
        cols = pl.ds(pl.multiple_of(n * tile, tile), tile)
        pre = product(lambda k0, depth: w_in[k0:k0 + depth, cols]) + b_in_of(cols).astype(F32)
        put(act_out, None, cols, jax.nn.gelu(pre, approximate=True).astype(BF16))
        return carry

    lax.fori_loop(0, w_in.shape[1] // tile, in_body, 0)


def first_kernel(x_ref, cos_ref, sin_ref, gain_ref, bias_ref, wq_ref, wk_ref, wv_ref, w_in_ref, b_in_ref,
                 qkv_ref, act_ref, normed, w_qkv, w_in, sems):
    step = pl.program_id(0)
    copies = [pltpu.make_async_copy(w.at[0], w_qkv.at[i], sems.at[i]) for i, w in enumerate((wq_ref, wk_ref, wv_ref))]
    copies.append(pltpu.make_async_copy(w_in_ref.at[0], w_in, sems.at[3]))

    @pl.when(step == 0)
    def _():
        for copy in copies:
            copy.start()

    gain, bias = gain_ref[0:1].astype(F32), bias_ref[0:1].astype(F32)
    group = 16

    def body(g, carry):
        rows = pl.ds(pl.multiple_of(g * group, group), group)
        normed[rows, :] = norm_rows(x_ref[rows, :].astype(F32), gain, bias)
        return carry

    lax.fori_loop(0, x_ref.shape[0] // group, body, 0)

    @pl.when(step == 0)
    def _():
        for copy in copies:
            copy.wait()

    depth = normed.shape[1] // STREAMS
    project(lambda i: normed[:, i * depth:(i + 1) * depth], [(0, normed.shape[0])],
            lambda: cos_ref[...], lambda: sin_ref[...], w_qkv, w_in, lambda cols: b_in_ref[0:1, cols], qkv_ref, act_ref)


def first_projection(x, cos, sin, ln_gain, ln_bias, w_q, w_k, w_v, w_in, b_in):
    rows, width = x.shape
    head, ff = w_q.shape[2], w_in.shape[2]
    block = 256
    whole = lambda a: pl.BlockSpec(a.shape, lambda g: (0,) * a.ndim)
    any_spec = pl.BlockSpec(memory_space=pl.ANY)
    return pl.pallas_call(
        first_kernel,
        grid=(rows // block,),
        in_specs=[pl.BlockSpec((block, width), lambda g: (g, 0)), pl.BlockSpec((block, 128), lambda g: (g, 0)),
                  pl.BlockSpec((block, 128), lambda g: (g, 0)), whole(ln_gain), whole(ln_bias),
                  any_spec, any_spec, any_spec, any_spec, whole(b_in)],
        out_specs=[pl.BlockSpec((3, block, head), lambda g: (0, g, 0)), pl.BlockSpec((block, ff), lambda g: (g, 0))],
        out_shape=[jax.ShapeDtypeStruct((3, rows, head), BF16), jax.ShapeDtypeStruct((rows, ff), BF16)],
        scratch_shapes=[pltpu.VMEM((block, width), BF16), pltpu.VMEM((3, width, head), BF16),
                        pltpu.VMEM((width, ff), BF16), pltpu.SemaphoreType.DMA((4,))],
        compiler_params=pltpu.CompilerParams(vmem_limit_bytes=VMEM_LIMIT, dimension_semantics=("arbitrary",)),
        name="first_projection",
    )(x, cos, sin, ln_gain, ln_bias, w_q, w_k, w_v, w_in, b_in)


def attend_kernel(pos_row_ref, pos_lane_ref, qkv_ref, k_ref, v_ref, *rest):
    ctx_ref, k_out_ref, v_out_ref = rest[-3:]
    steps, batch, dim = qkv_ref.shape[1:]
    slots = k_ref.shape[1]
    flat = lambda i: qkv_ref[i].astype(F32).reshape(steps * batch, dim).astype(BF16)
    query, key, value = flat(0), flat(1), flat(2)
    n_rows, n_cols = steps * batch, batch * slots
    place_row = lax.broadcasted_iota(jnp.int32, (n_cols, n_rows), 0)
    place_col = lax.broadcasted_iota(jnp.int32, (n_cols, n_rows), 1)
    hit = (lax.div(place_row, slots) == lax.rem(place_col, batch)) & (lax.rem(place_row, slots) == pos_lane_ref[0])
    one_hot = jnp.where(hit, 1.0, 0.0)
    written = jnp.sum(one_hot, axis=1, keepdims=True) > 0.5
    one_hot = one_hot.astype(BF16)
    caches = []
    for new, old_ref, out_ref in ((key, k_ref, k_out_ref), (value, v_ref, v_out_ref)):
        placed = jnp.dot(one_hot, new, preferred_element_type=F32)
        cache = jnp.where(written, placed, old_ref[...].reshape(n_cols, dim).astype(F32)).astype(BF16)
        out_ref[...] = cache.reshape(batch, slots, dim)
        caches.append(cache)
    scores = lax.dot_general(query, caches[0], (((1,), (1,)), ((), ())), preferred_element_type=F32) * (dim ** -0.5)
    row = lax.broadcasted_iota(jnp.int32, (n_rows, n_cols), 0)
    col = lax.broadcasted_iota(jnp.int32, (n_rows, n_cols), 1)
    visible = (lax.rem(row, batch) == lax.div(col, slots)) & (lax.rem(col, slots) <= pos_row_ref[0])
    scores = jnp.where(visible, scores, -jnp.inf)
    exp_scores = jnp.exp(scores - jnp.max(scores, axis=-1, keepdims=True))
    probs = (exp_scores / jnp.sum(exp_scores, axis=-1, keepdims=True)).astype(BF16)
    context = jnp.dot(probs, caches[1], preferred_element_type=F32)
    ctx_ref[...] = context.reshape(steps, batch, dim).astype(BF16)


def attention(layer, pos_row, pos_lane, qkv, k_cache, v_cache, carried):
    n_layers, batch, slots, dim = k_cache.shape
    steps = qkv.shape[1] // batch
    block = pos_row.shape[1] // steps
    cache_spec = pl.BlockSpec((None, block, slots, dim), lambda g: (layer, g, 0, 0))
    extra = list(carried)
    ctx, k_out, v_out = pl.pallas_call(
        attend_kernel,
        grid=(batch // block,),
        in_specs=[pl.BlockSpec((1,) + pos_row.shape[1:], lambda g: (g, 0, 0)),
                  pl.BlockSpec((1,) + pos_lane.shape[1:], lambda g: (g, 0, 0)),
                  pl.BlockSpec((3, steps, block, dim), lambda g: (0, 0, g, 0)), cache_spec, cache_spec]
        + [pl.BlockSpec(memory_space=pl.ANY)] * len(extra),
        out_specs=[pl.BlockSpec((steps, block, dim), lambda g: (0, g, 0)), cache_spec, cache_spec],
        out_shape=[jax.ShapeDtypeStruct((steps, batch, dim), BF16)] + [jax.ShapeDtypeStruct(k_cache.shape, BF16)] * 2,
        input_output_aliases={5: 1, 6: 2} if extra else {},
        compiler_params=pltpu.CompilerParams(vmem_limit_bytes=VMEM_LIMIT, dimension_semantics=("arbitrary",)),
        name=f"attention_{layer}",
    )(pos_row, pos_lane, qkv.reshape(3, steps, batch, dim), k_cache, v_cache, *extra)
    return ctx.reshape(steps * batch, dim), (k_out, v_out)


def sum_kernel(layer, last, *refs):
    if last:
        (ctx_ref, act_ref, hid_ref, b_out_ref, w_o_ref, w_out_ref,
         out_ref,
         w_cat, lhs, pbuf, sib_in, ring_in, full, hid, local_sem,
         sib_s, sib_r, ring_s, ring_r, ag_s, ag_r, agsib_s, agsib_r, put_sem) = refs
    else:
        (ctx_ref, act_ref, x_ref, b_out_ref, w_o_ref, w_out_ref,
         gain_ref, bias_ref, cos_ref, sin_ref, b_in_ref, wq_ref, wk_ref, wv_ref, w_in_ref,
         qkv_ref, act_out_ref, hid_ref,
         w_cat, lhs, pbuf, sib_in, ring_in, full, hid, local_sem,
         sib_s, sib_r, ring_s, ring_r, ag_s, ag_r, agsib_s, agsib_r,
         w_qkv, w_in, w_sem) = refs
    me = lax.axis_index("tp")
    chip, core = lax.div(me, 2), lax.rem(me, 2)
    pos = ring_of_chip(chip)
    right = {"tp": 2 * chip_of_ring(pos + 1) + core}
    left = {"tp": 2 * chip_of_ring(pos - 1) + core}
    sibling = {"tp": 2 * chip + 1 - core}
    chip_at = {off: chip_of_ring(pos + off) for off in OFFSETS}
    toward = (right, left)
    batch, part = pbuf.shape[3], pbuf.shape[4]
    pair = 2 * batch
    d_ctx = ctx_ref.shape[1]

    loads = []
    for i in range(STREAMS):
        cols = slice(i * part, (i + 1) * part)
        loads.append((pltpu.make_async_copy(w_o_ref.at[layer, :, cols], w_cat.at[i, 0:d_ctx, :], local_sem.at[2 * i]),
                      pltpu.make_async_copy(w_out_ref.at[layer, :, cols], w_cat.at[i, d_ctx:, :], local_sem.at[2 * i + 1])))
    for both in loads:
        for copy in both:
            copy.start()
    if last:
        own_load = pltpu.make_async_copy(hid_ref, hid, local_sem.at[2 * STREAMS])
    else:
        own_load = pltpu.make_async_copy(x_ref.at[me], hid, local_sem.at[2 * STREAMS])
        w_loads = [pltpu.make_async_copy(w.at[layer + 1], w_qkv.at[i], w_sem.at[i]) for i, w in enumerate((wq_ref, wk_ref, wv_ref))]
        w_loads.append(pltpu.make_async_copy(w_in_ref.at[layer + 1], w_in, w_sem.at[3]))
    own_load.start()

    barrier = pltpu.get_barrier_semaphore()
    for peer in (left, right, sibling):
        pl.semaphore_signal(barrier, inc=1, device_id=peer, device_id_type=pl.DeviceIdType.MESH)
    pl.semaphore_wait(barrier, 3)

    def remote(src, dst, send_sem, recv_sem, device):
        return pltpu.make_async_remote_copy(src_ref=src, dst_ref=dst, send_sem=send_sem, recv_sem=recv_sem,
                                            device_id=device, device_id_type=pl.DeviceIdType.MESH)

    def sib_copy(slot, i):
        return remote(pbuf.at[slot, i, 1 - core], sib_in.at[slot, i], sib_s.at[slot, i], sib_r.at[slot, i], sibling)

    def ring_copy(way, hop, i):
        slot = SLOT[4 - hop] if way == 0 else SLOT[hop - 4]
        return remote(pbuf.at[slot, i, core], ring_in.at[way, hop, i], ring_s.at[way, hop, i], ring_r.at[way, hop, i], toward[way])

    def gather_copy(way, hop, i):
        sign = -1 if way == 0 else 1
        src, dst = SLOT[sign * (hop - 1)], SLOT[sign * hop]
        return remote(full.at[i, src, core], full.at[i, dst, core], ag_s.at[way, hop - 1, i], ag_r.at[way, hop - 1, i], toward[way])

    def gather_sib(slot, i):
        return remote(full.at[i, slot, core], full.at[i, slot, core], agsib_s.at[slot, i], agsib_r.at[slot, i], sibling)

    def partials(offs):
        for j, off in enumerate(offs):
            rows = pl.ds(pl.multiple_of(chip_at[off] * pair, pair), pair)
            lhs[j * pair:(j + 1) * pair, :d_ctx] = ctx_ref[rows, :]
            lhs[j * pair:(j + 1) * pair, d_ctx:] = act_ref[rows, :]
        count = len(offs) * pair
        tile = min(256, part)
        for i in range(STREAMS):
            if offs[0] == 4:
                for copy in loads[i]:
                    copy.wait()

            def body(n, carry, i=i):
                cols = pl.ds(pl.multiple_of(n * tile, tile), tile)
                value = jnp.dot(lhs[:count, :], w_cat[i, :, cols], preferred_element_type=F32).astype(BF16)
                for j, off in enumerate(offs):
                    for c in range(2):
                        at = j * pair + c * batch
                        pbuf[SLOT[off], i, c, :, cols] = value[at:at + batch]
                return carry

            lax.fori_loop(0, part // tile, body, 0)
            for off in offs:
                sib_copy(SLOT[off], i).start()

    def add_up(slot, i, ring_terms):
        total = pbuf[slot, i, core].astype(F32) + sib_in[slot, i].astype(F32)
        for term in ring_terms:
            total = total + term.astype(F32)
        return total

    def has_fourth(way, i):
        return (i < STREAMS // 2) == (way == 0)

    partials([4])
    if not last:
        for copy in w_loads:
            copy.start()
    for i in range(STREAMS):
        sib_copy(7, i).wait_recv()
        pbuf[7, i, core] = add_up(7, i, []).astype(BF16)
        ring_copy(0 if has_fourth(0, i) else 1, 0, i).start()
    for hop in range(1, 4):
        partials([hop - 4, 4 - hop])
        order = (2, 3, 0, 1) if hop == 1 else (0, 1, 2, 3)
        for i in order:
            for way in range(2):
                k = i if way == 0 else STREAMS - 1 - i
                slot = SLOT[4 - hop] if way == 0 else SLOT[hop - 4]
                sib_copy(slot, k).wait_recv()
                terms = []
                if hop > 1 or has_fourth(way, k):
                    ring_copy(way, hop - 1, k).wait_recv()
                    terms.append(ring_in[way, hop - 1, k])
                pbuf[slot, k, core] = add_up(slot, k, terms).astype(BF16)
                ring_copy(way, hop, k).start()
    partials([0])
    own_load.wait()
    for i in range(STREAMS):
        cols = slice(i * part, (i + 1) * part)
        sib_copy(0, i).wait_recv()
        terms = []
        for way in range(2):
            ring_copy(way, 3, i).wait_recv()
            terms.append(ring_in[way, 3, i])
        total = hid[:, cols].astype(F32) + add_up(0, i, terms) + b_out_ref[layer:layer + 1, cols].astype(F32)
        hid[:, cols] = total.astype(BF16)
        if last:
            full[i, 0, core] = total.astype(BF16)
            for way in range(2):
                gather_copy(way, 1, i).start()
            gather_sib(0, i).start()
    if not last:
        gain, bias = gain_ref[layer + 1:layer + 2].astype(F32), bias_ref[layer + 1:layer + 2].astype(F32)
        group = 16

        def norm_body(g, carry):
            rows = pl.ds(pl.multiple_of(g * group, group), group)
            normed = norm_rows(hid[rows, :].astype(F32), gain, bias)
            for i in range(STREAMS):
                full[i, 0, core, rows, :] = normed[:, i * part:(i + 1) * part]
            return carry

        lax.fori_loop(0, batch // group, norm_body, 0)
        for i in range(STREAMS):
            for way in range(2):
                gather_copy(way, 1, i).start()
            gather_sib(0, i).start()
        hid_ref[...] = hid[...]
        for copy in w_loads:
            copy.wait()

    def use(offs):
        for off in offs:
            for i in range(STREAMS):
                gather_sib(SLOT[off], i).wait_recv()
        if last:
            for off in offs:
                for i in range(STREAMS):
                    put(off, i).start()
            return
        first, count = SLOT[offs[0]], len(offs)

        def table(ref):
            return jnp.concatenate([ref[pl.ds(pl.multiple_of(chip_at[off] * pair, pair), pair), :] for off in offs], axis=0)

        project(lambda i: full[i, first:first + count].reshape(count * pair, part),
                [(pl.multiple_of(chip_at[off] * pair, pair), pair) for off in offs],
                lambda: table(cos_ref), lambda: table(sin_ref), w_qkv, w_in, lambda cols: b_in_ref[layer + 1:layer + 2, cols],
                qkv_ref, act_out_ref)

    def put(off, i):
        slot = SLOT[off]
        return pltpu.make_async_copy(full.at[i, slot], out_ref.at[pl.ds(2 * chip_at[off], 2), :, i * part:(i + 1) * part], put_sem.at[slot, i])

    use([0])
    for hop in range(2, 5):
        for i in range(STREAMS):
            for way in range(2):
                k = i if way == 0 else STREAMS - 1 - i
                gather_copy(way, hop - 1, k).wait_recv()
                if hop < 4 or has_fourth(way, k):
                    gather_copy(way, hop, k).start()
                gather_sib(SLOT[1 - hop] if way == 0 else SLOT[hop - 1], k).start()
        use([1 - hop, hop - 1])
    for i in range(STREAMS):
        gather_copy(0 if has_fourth(0, i) else 1, 4, i).wait_recv()
        gather_sib(7, i).start()
    use([4])

    for i in range(STREAMS):
        for slot in range(CHIPS):
            sib_copy(slot, i).wait_send()
            gather_sib(slot, i).wait_send()
        for way in range(2):
            for hop in range(4):
                if hop > 0 or has_fourth(way, i):
                    ring_copy(way, hop, i).wait_send()
                if hop < 3 or has_fourth(way, i):
                    gather_copy(way, hop + 1, i).wait_send()
        if last:
            for off in OFFSETS:
                put(off, i).wait()


def sum_over_tp(layer, ctx, act, own, b_out, w_o, w_out, rest=None):
    rows, d_ctx = ctx.shape
    ff, width = act.shape[1], w_o.shape[2]
    batch, part = rows // TP, width // STREAMS
    last = rest is None
    vmem, hbm = pl.BlockSpec(memory_space=pltpu.VMEM), pl.BlockSpec(memory_space=pl.ANY)
    dma = pltpu.SemaphoreType.DMA
    scratch = [pltpu.VMEM((STREAMS, d_ctx + ff, part), BF16), pltpu.VMEM((4 * batch, d_ctx + ff), BF16),
               pltpu.VMEM((CHIPS, STREAMS, 2, batch, part), BF16), pltpu.VMEM((CHIPS, STREAMS, batch, part), BF16),
               pltpu.VMEM((2, 4, STREAMS, batch, part), BF16), pltpu.VMEM((STREAMS, CHIPS, 2, batch, part), BF16),
               pltpu.VMEM((batch, width), BF16), dma((2 * STREAMS + 1,)),
               dma((CHIPS, STREAMS)), dma((CHIPS, STREAMS)), dma((2, 4, STREAMS)), dma((2, 4, STREAMS)),
               dma((2, 4, STREAMS)), dma((2, 4, STREAMS)), dma((CHIPS, STREAMS)), dma((CHIPS, STREAMS))]
    params = pltpu.CompilerParams(collective_id=layer, has_side_effects=True, vmem_limit_bytes=VMEM_LIMIT)
    if last:
        return pl.pallas_call(
            functools.partial(sum_kernel, layer, True),
            in_specs=[vmem, vmem, hbm, vmem, hbm, hbm],
            out_specs=hbm,
            out_shape=jax.ShapeDtypeStruct((TP, batch, width), BF16),
            scratch_shapes=scratch + [dma((CHIPS, STREAMS))],
            compiler_params=params, name=f"sum_{layer}",
        )(ctx, act, own, b_out, w_o, w_out)
    gain, bias, cos, sin, b_in, w_q, w_k, w_v, w_in = rest
    return pl.pallas_call(
        functools.partial(sum_kernel, layer, False),
        in_specs=[vmem, vmem, hbm, vmem, hbm, hbm, vmem, vmem, vmem, vmem, vmem, hbm, hbm, hbm, hbm],
        out_specs=[vmem, vmem, vmem],
        out_shape=[jax.ShapeDtypeStruct((3, rows, d_ctx), BF16), jax.ShapeDtypeStruct((rows, ff), BF16),
                   jax.ShapeDtypeStruct((batch, width), BF16)],
        scratch_shapes=scratch + [pltpu.VMEM((3, width, d_ctx), BF16), pltpu.VMEM((width, ff), BF16), dma((4,))],
        compiler_params=params, name=f"sum_{layer}",
    )(ctx, act, own, b_out, w_o, w_out, gain, bias, cos, sin, b_in, w_q, w_k, w_v, w_in)


def rotary_tables(positions):
    inv_freq = 1.0 / (10000.0 ** (jnp.arange(0, ROT_DIM, 2).astype(F32) / ROT_DIM))
    angles = positions.astype(F32)[:, None] * inv_freq[None, :]
    cos = jnp.repeat(jnp.cos(angles), 2, axis=1)
    sin = jnp.repeat(jnp.sin(angles), 2, axis=1) * jnp.where(jnp.arange(ROT_DIM) % 2 == 0, -1.0, 1.0)
    rest = 128 - ROT_DIM
    return jnp.pad(cos, ((0, 0), (0, rest)), constant_values=1.0), jnp.pad(sin, ((0, 0), (0, rest)))


def decode_shard(x_steps, cur_len, k_cache, v_cache, ln_gain, ln_bias, w_q, w_k, w_v, w_o, w_in, b_in, w_out, b_out):
    n_layers, batch, slots, _, dim = k_cache.shape
    steps, _, width = x_steps.shape
    rows = steps * batch
    pos = cur_len[None, :] + jnp.arange(steps, dtype=jnp.int32)[:, None]
    cos, sin = rotary_tables(pos.reshape(rows))
    block = 8
    grouped = pos.reshape(steps, batch // block, block).transpose(1, 0, 2).reshape(batch // block, steps * block)
    pos_row, pos_lane = grouped[:, :, None], grouped[:, None, :]
    k_old, v_old = k_cache.reshape(n_layers, batch, slots, dim), v_cache.reshape(n_layers, batch, slots, dim)

    qkv, act = first_projection(x_steps.reshape(rows, width), cos, sin, ln_gain, ln_bias, w_q, w_k, w_v, w_in, b_in)
    ctx, caches = attention(0, pos_row, pos_lane, qkv, k_old, v_old, ())
    qkv, act, own = sum_over_tp(0, ctx, act, x_steps, b_out, w_o, w_out,
                                (ln_gain, ln_bias, cos, sin, b_in, w_q, w_k, w_v, w_in))
    ctx, caches = attention(1, pos_row, pos_lane, qkv, k_old, v_old, caches)
    hidden = sum_over_tp(1, ctx, act, own, b_out, w_o, w_out)
    return hidden, caches[0].reshape(k_cache.shape), caches[1].reshape(v_cache.shape)


def solution(mesh):
    cache_spec = P(None, "dp", None, "tp", None)
    in_specs = (P(None, "dp", None), P("dp"), cache_spec, cache_spec, P(None, None), P(None, None),
                P(None, None, "tp"), P(None, None, "tp"), P(None, None, "tp"), P(None, "tp", None),
                P(None, None, "tp"), P(None, "tp"), P(None, "tp", None), P(None, None))
    out_specs = (P(None, "dp", None), cache_spec, cache_spec)
    return jax.shard_map(decode_shard, mesh=mesh, in_specs=in_specs, out_specs=out_specs, check_vma=False)
```

time: 2840 us -> 285 us (0.10)
  waiting for transfers between devices: 1480 us -> 0 us
  matrix products: 665 us -> 0 us
  local copies, waits for them, and re-layouts: 568 us -> 11.7 us
  Pallas kernels: 0 us -> 269 us
  other arithmetic: 84.7 us -> 2.74 us
    psum x17 -> x0, waiting for transfers between devices: 1480 us -> none  [decode_shard(): layer_sum = lax.psum(layer_part.astype(jnp.bfloat16), 'tp')]
    dot_general x224 -> x0, matrix products: 665 us -> none  [the longest x32 307 us: layer_update(): jnp.dot(gelu_act, out_weight, preferred_element_type=jnp.float32)]
    scatter x64 -> x0, local copies, waits for them, and re-layouts: 519 us -> none  [the longest x32 261 us: layer_update(): v_cache = v_cache.at[layer_idx, batch_rows, new_pos].set(value_new)]
    pallas_call x0 -> x5, Pallas kernels: none -> 269 us  [the longest x1 109 us: sum_over_tp(): pl.pallas_call(functools.partial(sum_kernel, layer, False), in_specs=[vme...]
    reduce_sum x67 -> x0, other arithmetic: 44.7 us -> none  [the longest x17 28.6 us: layer_norm(): row_mean = jnp.mean(hid_f32, axis=-1, keepdims=True)]
  transfers between devices with their start and end apart: 17 -> 0, of which waited for: 16 -> 0; matrix products, arithmetic and copies ran while one was open for 11% -> 0% of each run, Pallas kernels for 0% -> 0%
where the time goes in v2:
time: 285 us; the launch traced here: 284 us
  Pallas kernels  269 us (94%)
  local copies, waits for them, and re-layouts  11.7 us (4%)
    pallas_call x1, Pallas kernels, sum_over_tp(): pl.pallas_call(functools.partial(sum_kernel, layer, False), in_specs=[vme...  109 us
    pallas_call x1, Pallas kernels, sum_over_tp(): pl.pallas_call(functools.partial(sum_kernel, layer, True), in_specs=[vmem...  98.5 us
    pallas_call x1, Pallas kernels, first_projection(): pl.pallas_call(first_kernel, grid=(rows // block,), in_specs=[pl.BlockSpe...  43 us
    pallas_call x2, Pallas kernels, attention(): pl.pallas_call(attend_kernel, grid=(batch // block,), in_specs=[pl.BlockS...  18.9 us
    unnamed x1, local copies, waits for them, and re-layouts  7.89 us

profile of v2, /device:TPU:0, one launch (start us, length us, event | category | flops | bytes accessed | tf_op | source)
XLA Modules:
  0.0 284.0 jit_solution(5476027010157490350)
XLA Ops:
  0.7 0.7 add.69
  1.4 0.7 add_convert_fusion
  2.1 0.1 convert_element_type.20
  2.1 0.1 add.73
  2.2 0.1 add.76
  2.3 0.6 broadcast_add_fusion.1.pos_lane_ref
  2.9 0.5 multiply_sine_fusion
  3.5 0.1 broadcast_in_dim.20
  3.6 0.2 reshape.133
  3.7 0.2 copy.30
  4.0 0.8 pad.9.sin_ref.refs_9_
  4.8 0.1 broadcast_in_dim.19
  4.9 0.2 reshape.132
  5.1 0.2 copy.29
  5.3 0.8 pad.8.cos_ref.refs_8_
  6.2 0.2 add.83
  6.3 0.9 broadcast_add_fusion.pos_row_ref
  7.2 43.0 %first_projection.1 = (bf16[3,1024,256]{2,1,0:T(8,128)(2,1)}, bf16[1024,1024]{1,0:T(8,128)(2,1)}) custom-call(bf16[1024,4096]{1,0:T(8,128)(2,1)} %bitcast.18, f32[1024,128]{1,0:T(8,128)} %pad.8.cos_ref.refs_8_, f32[1024,128]{1,0:T(8,128)} %pad.9.sin_ref.refs_9_, bf16[2,4096]{1,0:T(2,128)(2,1)} %refs_6_.1, bf16[2,4096]{1,0:T(2,128)(2,1)} %refs_7_.1, ...), custom_call_target="tpu_custom_call" | custom-call | tf_op jit(solution)/shard_map/first_projection/pallas_call | solution.py:122
  50.3 9.5 %attention_0.1 = (bf16[16,64,256]{2,1,0:T(8,128)(2,1)}, bf16[2,64,64,256]{3,2,1,0:T(8,128)(2,1)}, bf16[2,64,64,256]{3,2,1,0:T(8,128)(2,1)}) custom-call(s32[8,128,1]{2,1,0:T(8,128)} %broadcast_add_fusion.pos_row_ref, s32[8,1,128]{2,1,0:T(1,128)} %broadcast_add_fusion.1.pos_lane_ref, bf16[3,16,64,256]{3,2,1,0:T(8,128)(2,1)} %bitcast.26, ...), custom_call_target="tpu_custom_call" | custom-call | tf_op jit(solution)/shard_map/attention_0/pallas_call | solution.py:173
  59.8 108.5 %sum_0.1 = (bf16[3,1024,256]{2,1,0:T(8,128)(2,1)}, bf16[1024,1024]{1,0:T(8,128)(2,1)}, bf16[64,4096]{1,0:T(8,128)(2,1)}) custom-call(bf16[1024,256]{1,0:T(8,128)(2,1)} %bitcast.27, bf16[1024,1024]{1,0:T(8,128)(2,1)} %get-tuple-element.16.refs_1_, bf16[16,64,4096]{2,1,0:T(8,128)(2,1)} %refs_2_.1, bf16[2,4096]{1,0:T(2,128)(2,1)} %refs_3_.3, ...), custom_call_target="tpu_custom_call" | custom-call | tf_op jit(solution)/shard_map/sum_0/pallas_call | solution.py:423
  168.3 9.4 %attention_1.1 = (bf16[16,64,256]{2,1,0:T(8,128)(2,1)}, bf16[2,64,64,256]{3,2,1,0:T(8,128)(2,1)}, bf16[2,64,64,256]{3,2,1,0:T(8,128)(2,1)}) custom-call(s32[8,128,1]{2,1,0:T(8,128)} %broadcast_add_fusion.pos_row_ref, s32[8,1,128]{2,1,0:T(1,128)} %broadcast_add_fusion.1.pos_lane_ref, ...), custom_call_target="tpu_custom_call", output_to_operand_aliasing={{1}: (5, {}), {2}: (6, {})} | custom-call | tf_op jit(solution)/shard_map/attention_1/pallas_call | solution.py:173
  177.7 98.5 %sum_1.1 = bf16[16,64,4096]{2,1,0:T(8,128)(2,1)} custom-call(bf16[1024,256]{1,0:T(8,128)(2,1)} %bitcast.28, bf16[1024,1024]{1,0:T(8,128)(2,1)} %get-tuple-element.21.refs_1_, bf16[64,4096]{1,0:T(8,128)(2,1)} %get-tuple-element.22.refs_2_, bf16[2,4096]{1,0:T(2,128)(2,1)} %refs_3_.3, bf16[2,256,4096]{2,1,0:T(8,128)(2,1)} %refs_4_.3, bf16[2,1024,4096]{2,1,0:T(8,128)(2,1)} %refs_5_.3), custom_call_target="tpu_custom_call" | custom-call | tf_op jit(solution)/shard_map/sum_1/pallas_call | solution.py:414
  276.1 7.9 %copy.37 = bf16[16,64,4096]{2,1,0:T(8,128)(2,1)} copy(bf16[16,64,4096]{2,1,0:T(8,128)(2,1)} %sum_1.1) | data formatting | bytes 16777216
  (5 shorter events, 0.1 us)

commit v3 on v2

--- a/solution.py
+++ b/solution.py
@@ -2,6 +2,7 @@
 
 import jax
 import jax.numpy as jnp
+import numpy as np
 from jax import lax
 from jax.experimental import pallas as pl
 from jax.experimental.pallas import tpu as pltpu
@@ -31,11 +32,21 @@
     return 2 * z + y
 
 
-def norm_rows(x, gain, bias):
-    mean = jnp.mean(x, axis=-1, keepdims=True)
-    centered = x - mean
-    var = jnp.mean(centered * centered, axis=-1, keepdims=True)
-    return (centered * lax.rsqrt(var + LN_EPS) * gain + bias).astype(BF16)
+def norm_rows(load, store, gain_ref, bias_ref, layer, width):
+    starts = range(0, width, 128)
+    total = load(0).astype(F32)
+    for col in starts[1:]:
+        total = total + load(col).astype(F32)
+    mean = jnp.sum(total, axis=-1, keepdims=True) * (1.0 / width)
+    square = jnp.zeros_like(total)
+    for col in starts:
+        centered = load(col).astype(F32) - mean
+        square = square + centered * centered
+    scale = lax.rsqrt(jnp.sum(square, axis=-1, keepdims=True) * (1.0 / width) + LN_EPS)
+    for col in starts:
+        gain = gain_ref[layer:layer + 1, col:col + 128].astype(F32)
+        bias = bias_ref[layer:layer + 1, col:col + 128].astype(F32)
+        store(col, ((load(col).astype(F32) - mean) * scale * gain + bias).astype(BF16))
 
 
 def rotate(vec, cos, sin):
@@ -71,7 +82,7 @@
 
     lax.fori_loop(0, 2, qk_body, 0)
     put(qkv_out, 2, slice(None), product(lambda k0, depth: w_qkv[2, k0:k0 + depth, :]).astype(BF16))
-    tile = min(256, w_in.shape[1])
+    tile = min(512, w_in.shape[1])
 
     def in_body(n, carry):
         cols = pl.ds(pl.multiple_of(n * tile, tile), tile)
@@ -93,12 +104,15 @@
         for copy in copies:
             copy.start()
 
-    gain, bias = gain_ref[0:1].astype(F32), bias_ref[0:1].astype(F32)
-    group = 16
+    group = 64
 
     def body(g, carry):
         rows = pl.ds(pl.multiple_of(g * group, group), group)
-        normed[rows, :] = norm_rows(x_ref[rows, :].astype(F32), gain, bias)
+
+        def store(col, value):
+            normed[rows, col:col + 128] = value
+
+        norm_rows(lambda col: x_ref[rows, col:col + 128], store, gain_ref, bias_ref, 0, normed.shape[1])
         return carry
 
     lax.fori_loop(0, x_ref.shape[0] // group, body, 0)
@@ -116,7 +130,7 @@
 def first_projection(x, cos, sin, ln_gain, ln_bias, w_q, w_k, w_v, w_in, b_in):
     rows, width = x.shape
     head, ff = w_q.shape[2], w_in.shape[2]
-    block = 256
+    block = 512 if rows % 512 == 0 else 256
     whole = lambda a: pl.BlockSpec(a.shape, lambda g: (0,) * a.ndim)
     any_spec = pl.BlockSpec(memory_space=pl.ANY)
     return pl.pallas_call(
@@ -143,7 +157,8 @@
     n_rows, n_cols = steps * batch, batch * slots
     place_row = lax.broadcasted_iota(jnp.int32, (n_cols, n_rows), 0)
     place_col = lax.broadcasted_iota(jnp.int32, (n_cols, n_rows), 1)
-    hit = (lax.div(place_row, slots) == lax.rem(place_col, batch)) & (lax.rem(place_row, slots) == pos_lane_ref[0])
+    log = slots.bit_length() - 1
+    hit = ((place_row >> log) == (place_col & (batch - 1))) & ((place_row & (slots - 1)) == pos_lane_ref[0])
     one_hot = jnp.where(hit, 1.0, 0.0)
     written = jnp.sum(one_hot, axis=1, keepdims=True) > 0.5
     one_hot = one_hot.astype(BF16)
@@ -156,7 +171,7 @@
     scores = lax.dot_general(query, caches[0], (((1,), (1,)), ((), ())), preferred_element_type=F32) * (dim ** -0.5)
     row = lax.broadcasted_iota(jnp.int32, (n_rows, n_cols), 0)
     col = lax.broadcasted_iota(jnp.int32, (n_rows, n_cols), 1)
-    visible = (lax.rem(row, batch) == lax.div(col, slots)) & (lax.rem(col, slots) <= pos_row_ref[0])
+    visible = ((row & (batch - 1)) == (col >> log)) & ((col & (slots - 1)) <= pos_row_ref[0])
     scores = jnp.where(visible, scores, -jnp.inf)
     exp_scores = jnp.exp(scores - jnp.max(scores, axis=-1, keepdims=True))
     probs = (exp_scores / jnp.sum(exp_scores, axis=-1, keepdims=True)).astype(BF16)
@@ -190,8 +205,8 @@
     if last:
         (ctx_ref, act_ref, hid_ref, b_out_ref, w_o_ref, w_out_ref,
          out_ref,
-         w_cat, lhs, pbuf, sib_in, ring_in, full, hid, local_sem,
-         sib_s, sib_r, ring_s, ring_r, ag_s, ag_r, agsib_s, agsib_r, put_sem) = refs
+         w_cat, lhs, pbuf, sib_in, ring_in, hid, local_sem,
+         sib_s, sib_r, ring_s, ring_r, ag_s, ag_r, agsib_s, agsib_r) = refs
     else:
         (ctx_ref, act_ref, x_ref, b_out_ref, w_o_ref, w_out_ref,
          gain_ref, bias_ref, cos_ref, sin_ref, b_in_ref, wq_ref, wk_ref, wv_ref, w_in_ref,
@@ -243,21 +258,26 @@
         slot = SLOT[4 - hop] if way == 0 else SLOT[hop - 4]
         return remote(pbuf.at[slot, i, core], ring_in.at[way, hop, i], ring_s.at[way, hop, i], ring_r.at[way, hop, i], toward[way])
 
+    def landing(off, i):
+        return out_ref.at[2 * chip_at[off] + core, :, i * part:(i + 1) * part] if last else full.at[i, SLOT[off], core]
+
     def gather_copy(way, hop, i):
         sign = -1 if way == 0 else 1
-        src, dst = SLOT[sign * (hop - 1)], SLOT[sign * hop]
-        return remote(full.at[i, src, core], full.at[i, dst, core], ag_s.at[way, hop - 1, i], ag_r.at[way, hop - 1, i], toward[way])
+        src = landing(sign * (hop - 1), i)
+        dst = src if last else landing(sign * hop, i)
+        return remote(src, dst, ag_s.at[way, hop - 1, i], ag_r.at[way, hop - 1, i], toward[way])
 
     def gather_sib(slot, i):
-        return remote(full.at[i, slot, core], full.at[i, slot, core], agsib_s.at[slot, i], agsib_r.at[slot, i], sibling)
-
-    def partials(offs):
+        off = OFFSETS[slot]
+        return remote(landing(off, i), landing(off, i), agsib_s.at[slot, i], agsib_r.at[slot, i], sibling)
+
+    def partials(offs, then=None):
         for j, off in enumerate(offs):
             rows = pl.ds(pl.multiple_of(chip_at[off] * pair, pair), pair)
             lhs[j * pair:(j + 1) * pair, :d_ctx] = ctx_ref[rows, :]
             lhs[j * pair:(j + 1) * pair, d_ctx:] = act_ref[rows, :]
         count = len(offs) * pair
-        tile = min(256, part)
+        tile = min(512, part)
         for i in range(STREAMS):
             if offs[0] == 4:
                 for copy in loads[i]:
@@ -275,6 +295,10 @@
             lax.fori_loop(0, part // tile, body, 0)
             for off in offs:
                 sib_copy(SLOT[off], i).start()
+            if then is not None and i > 0:
+                then(i - 1)
+        if then is not None:
+            then(STREAMS - 1)
 
     def add_up(slot, i, ring_terms):
         total = pbuf[slot, i, core].astype(F32) + sib_in[slot, i].astype(F32)
@@ -285,28 +309,31 @@
     def has_fourth(way, i):
         return (i < STREAMS // 2) == (way == 0)
 
-    partials([4])
+    def start_ring(i):
+        sib_copy(7, i).wait_recv()
+        pbuf[7, i, core] = add_up(7, i, []).astype(BF16)
+        ring_copy(0 if has_fourth(0, i) else 1, 0, i).start()
+
+    def pass_on(hop, i):
+        for way in range(2):
+            k = i if way == 0 else STREAMS - 1 - i
+            slot = SLOT[4 - hop] if way == 0 else SLOT[hop - 4]
+            sib_copy(slot, k).wait_recv()
+            terms = []
+            if hop > 1 or has_fourth(way, k):
+                ring_copy(way, hop - 1, k).wait_recv()
+                terms.append(ring_in[way, hop - 1, k])
+            pbuf[slot, k, core] = add_up(slot, k, terms).astype(BF16)
+            ring_copy(way, hop, k).start()
+
+    partials([4], start_ring)
     if not last:
         for copy in w_loads:
             copy.start()
-    for i in range(STREAMS):
-        sib_copy(7, i).wait_recv()
-        pbuf[7, i, core] = add_up(7, i, []).astype(BF16)
-        ring_copy(0 if has_fourth(0, i) else 1, 0, i).start()
     for hop in range(1, 4):
         partials([hop - 4, 4 - hop])
-        order = (2, 3, 0, 1) if hop == 1 else (0, 1, 2, 3)
-        for i in order:
-            for way in range(2):
-                k = i if way == 0 else STREAMS - 1 - i
-                slot = SLOT[4 - hop] if way == 0 else SLOT[hop - 4]
-                sib_copy(slot, k).wait_recv()
-                terms = []
-                if hop > 1 or has_fourth(way, k):
-                    ring_copy(way, hop - 1, k).wait_recv()
-                    terms.append(ring_in[way, hop - 1, k])
-                pbuf[slot, k, core] = add_up(slot, k, terms).astype(BF16)
-                ring_copy(way, hop, k).start()
+        for i in (2, 3, 0, 1) if hop == 1 else (0, 1, 2, 3):
+            pass_on(hop, i)
     partials([0])
     own_load.wait()
     for i in range(STREAMS):
@@ -317,24 +344,19 @@
             ring_copy(way, 3, i).wait_recv()
             terms.append(ring_in[way, 3, i])
         total = hid[:, cols].astype(F32) + add_up(0, i, terms) + b_out_ref[layer:layer + 1, cols].astype(F32)
-        hid[:, cols] = total.astype(BF16)
+        if not last:
+            hid[:, cols] = total.astype(BF16)
         if last:
-            full[i, 0, core] = total.astype(BF16)
+            out_ref[me, :, cols] = total.astype(BF16)
             for way in range(2):
                 gather_copy(way, 1, i).start()
             gather_sib(0, i).start()
     if not last:
-        gain, bias = gain_ref[layer + 1:layer + 2].astype(F32), bias_ref[layer + 1:layer + 2].astype(F32)
-        group = 16
-
-        def norm_body(g, carry):
-            rows = pl.ds(pl.multiple_of(g * group, group), group)
-            normed = norm_rows(hid[rows, :].astype(F32), gain, bias)
-            for i in range(STREAMS):
-                full[i, 0, core, rows, :] = normed[:, i * part:(i + 1) * part]
-            return carry
-
-        lax.fori_loop(0, batch // group, norm_body, 0)
+        def store(col, value):
+            at = col % part
+            full[col // part, 0, core, :, at:at + 128] = value
+
+        norm_rows(lambda col: hid[:, col:col + 128], store, gain_ref, bias_ref, layer + 1, STREAMS * part)
         for i in range(STREAMS):
             for way in range(2):
                 gather_copy(way, 1, i).start()
@@ -348,9 +370,6 @@
             for i in range(STREAMS):
                 gather_sib(SLOT[off], i).wait_recv()
         if last:
-            for off in offs:
-                for i in range(STREAMS):
-                    put(off, i).start()
             return
         first, count = SLOT[offs[0]], len(offs)
 
@@ -361,10 +380,6 @@
                 [(pl.multiple_of(chip_at[off] * pair, pair), pair) for off in offs],
                 lambda: table(cos_ref), lambda: table(sin_ref), w_qkv, w_in, lambda cols: b_in_ref[layer + 1:layer + 2, cols],
                 qkv_ref, act_out_ref)
-
-    def put(off, i):
-        slot = SLOT[off]
-        return pltpu.make_async_copy(full.at[i, slot], out_ref.at[pl.ds(2 * chip_at[off], 2), :, i * part:(i + 1) * part], put_sem.at[slot, i])
 
     use([0])
     for hop in range(2, 5):
@@ -391,9 +406,6 @@
                     ring_copy(way, hop, i).wait_send()
                 if hop < 3 or has_fourth(way, i):
                     gather_copy(way, hop + 1, i).wait_send()
-        if last:
-            for off in OFFSETS:
-                put(off, i).wait()
 
 
 def sum_over_tp(layer, ctx, act, own, b_out, w_o, w_out, rest=None):
@@ -405,18 +417,22 @@
     dma = pltpu.SemaphoreType.DMA
     scratch = [pltpu.VMEM((STREAMS, d_ctx + ff, part), BF16), pltpu.VMEM((4 * batch, d_ctx + ff), BF16),
                pltpu.VMEM((CHIPS, STREAMS, 2, batch, part), BF16), pltpu.VMEM((CHIPS, STREAMS, batch, part), BF16),
-               pltpu.VMEM((2, 4, STREAMS, batch, part), BF16), pltpu.VMEM((STREAMS, CHIPS, 2, batch, part), BF16),
+               pltpu.VMEM((2, 4, STREAMS, batch, part), BF16)]
+    if not last:
+        scratch.append(pltpu.VMEM((STREAMS, CHIPS, 2, batch, part), BF16))
+    scratch += [
                pltpu.VMEM((batch, width), BF16), dma((2 * STREAMS + 1,)),
                dma((CHIPS, STREAMS)), dma((CHIPS, STREAMS)), dma((2, 4, STREAMS)), dma((2, 4, STREAMS)),
                dma((2, 4, STREAMS)), dma((2, 4, STREAMS)), dma((CHIPS, STREAMS)), dma((CHIPS, STREAMS))]
-    params = pltpu.CompilerParams(collective_id=layer, has_side_effects=True, vmem_limit_bytes=VMEM_LIMIT)
+    params = pltpu.CompilerParams(collective_id=layer, has_side_effects=True,
+                                  vmem_limit_bytes=VMEM_LIMIT - 2 * TP * batch * width if last else VMEM_LIMIT)
     if last:
         return pl.pallas_call(
             functools.partial(sum_kernel, layer, True),
             in_specs=[vmem, vmem, hbm, vmem, hbm, hbm],
-            out_specs=hbm,
-            out_shape=jax.ShapeDtypeStruct((TP, batch, width), BF16),
-            scratch_shapes=scratch + [dma((CHIPS, STREAMS))],
+            out_specs=vmem,
+            out_shape=pltpu.VMEM((TP, batch, width), BF16),
+            scratch_shapes=scratch,
             compiler_params=params, name=f"sum_{layer}",
         )(ctx, act, own, b_out, w_o, w_out)
     gain, bias, cos, sin, b_in, w_q, w_k, w_v, w_in = rest
@@ -432,12 +448,13 @@
 
 
 def rotary_tables(positions):
-    inv_freq = 1.0 / (10000.0 ** (jnp.arange(0, ROT_DIM, 2).astype(F32) / ROT_DIM))
+    lane = np.arange(128)
+    exponent = (lane // 2 * 2).astype(np.float32) / ROT_DIM
+    turned = lane < ROT_DIM
+    inv_freq = jnp.where(turned, 1.0 / (10000.0 ** jnp.asarray(exponent, F32)), 0.0)
+    sign = np.where(turned, np.where(lane % 2 == 0, -1.0, 1.0), 0.0).astype(np.float32)
     angles = positions.astype(F32)[:, None] * inv_freq[None, :]
-    cos = jnp.repeat(jnp.cos(angles), 2, axis=1)
-    sin = jnp.repeat(jnp.sin(angles), 2, axis=1) * jnp.where(jnp.arange(ROT_DIM) % 2 == 0, -1.0, 1.0)
-    rest = 128 - ROT_DIM
-    return jnp.pad(cos, ((0, 0), (0, rest)), constant_values=1.0), jnp.pad(sin, ((0, 0), (0, rest)))
+    return jnp.cos(angles), jnp.sin(angles) * sign
 
 
 def decode_shard(x_steps, cur_len, k_cache, v_cache, ln_gain, ln_bias, w_q, w_k, w_v, w_o, w_in, b_in, w_out, b_out):

time: 285 us -> 263 us (0.923)
  Pallas kernels: 269 us -> 251 us
  local copies, waits for them, and re-layouts: 11.7 us -> 4.57 us
  other arithmetic: 2.74 us -> 5.91 us
    pallas_call x1, Pallas kernels: 43 us -> 31.8 us  [first_projection(): pl.pallas_call(first_kernel, grid=(rows // block,), in_specs=[pl.BlockSpe...]
    unnamed x1, local copies, waits for them, and re-layouts: 7.89 us -> 3.4 us
    mul x1, other arithmetic: 0.04 us -> 3.75 us  [rotary_tables(): return (jnp.cos(angles), jnp.sin(angles) * sign)]
    pallas_call x1, Pallas kernels: 98.5 us -> 95.3 us  [sum_over_tp(): pl.pallas_call(functools.partial(sum_kernel, layer, True), in_specs=[vmem...]
    pallas_call x1, Pallas kernels: 109 us -> 106 us  [sum_over_tp(): pl.pallas_call(functools.partial(sum_kernel, layer, False), in_specs=[vme...]
where the time goes in v3:
time: 263 us
  Pallas kernels  251 us (95%)
  other arithmetic  5.91 us (2%)
  local copies, waits for them, and re-layouts  4.57 us (2%)
    pallas_call x1, Pallas kernels, sum_over_tp(): pl.pallas_call(functools.partial(sum_kernel, layer, False), in_specs=[vme...  106 us
    pallas_call x1, Pallas kernels, sum_over_tp(): pl.pallas_call(functools.partial(sum_kernel, layer, True), in_specs=[vmem...  95.3 us
    pallas_call x1, Pallas kernels, first_projection(): pl.pallas_call(first_kernel, grid=(rows // block,), in_specs=[pl.BlockSpe...  31.8 us
    pallas_call x2, Pallas kernels, attention(): pl.pallas_call(attend_kernel, grid=(batch // block,), in_specs=[pl.BlockS...  18.9 us

profile of v3, /device:TPU:0, one launch (start us, length us, event | category | flops | bytes accessed | tf_op | source)
XLA Modules:
  0.0 262.6 jit_solution(18367508737153269463)
XLA Ops:
  0.6 0.7 add.55
  1.4 0.7 add_convert_fusion
  2.0 0.1 convert_element_type.11
  2.1 0.1 add.59
  2.2 0.1 add.62
  2.3 0.6 broadcast_add_fusion.1.pos_lane_ref
  2.9 0.2 add.68
  3.1 0.9 broadcast_add_fusion.pos_row_ref
  4.0 3.8 %fusion = (f32[1024,128]{1,0:T(8,128)}, f32[1024,128]{1,0:T(8,128)}) fusion(f32[128]{0:T(128)} %constant.13.clone, f32[128]{0:T(128)} %constant.18, f32[1024]{0:T(1024)S(1)} %convert_element_type.11), kind=kLoop, calls=%fused_computation.2 | loop fusion | flops 262144 | bytes 1053696 | tf_op jit(solution)/shard_map/mul | solution.py:457
  7.7 31.8 %first_projection.1 = (bf16[3,1024,256]{2,1,0:T(8,128)(2,1)}, bf16[1024,1024]{1,0:T(8,128)(2,1)}) custom-call(bf16[1024,4096]{1,0:T(8,128)(2,1)} %bitcast.14, f32[1024,128]{1,0:T(8,128)} %get-tuple-element.32.cos_ref.refs_8_, f32[1024,128]{1,0:T(8,128)} %get-tuple-element.31.sin_ref.refs_9_, bf16[2,4096]{1,0:T(2,128)(2,1)} %refs_6_.1, ...), custom_call_target="tpu_custom_call" | custom-call | tf_op jit(solution)/shard_map/first_projection/pallas_call | solution.py:136
  39.5 9.5 %attention_0.1 = (bf16[16,64,256]{2,1,0:T(8,128)(2,1)}, bf16[2,64,64,256]{3,2,1,0:T(8,128)(2,1)}, bf16[2,64,64,256]{3,2,1,0:T(8,128)(2,1)}) custom-call(s32[8,128,1]{2,1,0:T(8,128)} %broadcast_add_fusion.pos_row_ref, s32[8,1,128]{2,1,0:T(1,128)} %broadcast_add_fusion.1.pos_lane_ref, bf16[3,16,64,256]{3,2,1,0:T(8,128)(2,1)} %bitcast.22, ...), custom_call_target="tpu_custom_call" | custom-call | tf_op jit(solution)/shard_map/attention_0/pallas_call | solution.py:188
  49.0 105.5 %sum_0.1 = (bf16[3,1024,256]{2,1,0:T(8,128)(2,1)}, bf16[1024,1024]{1,0:T(8,128)(2,1)}, bf16[64,4096]{1,0:T(8,128)(2,1)}) custom-call(bf16[1024,256]{1,0:T(8,128)(2,1)} %bitcast.23, bf16[1024,1024]{1,0:T(8,128)(2,1)} %get-tuple-element.16.refs_1_, bf16[16,64,4096]{2,1,0:T(8,128)(2,1)} %refs_2_.1, bf16[2,4096]{1,0:T(2,128)(2,1)} %refs_3_.3, ...), custom_call_target="tpu_custom_call" | custom-call | tf_op jit(solution)/shard_map/sum_0/pallas_call | solution.py:439
  154.6 9.4 %attention_1.1 = (bf16[16,64,256]{2,1,0:T(8,128)(2,1)}, bf16[2,64,64,256]{3,2,1,0:T(8,128)(2,1)}, bf16[2,64,64,256]{3,2,1,0:T(8,128)(2,1)}) custom-call(s32[8,128,1]{2,1,0:T(8,128)} %broadcast_add_fusion.pos_row_ref, s32[8,1,128]{2,1,0:T(1,128)} %broadcast_add_fusion.1.pos_lane_ref, ...), custom_call_target="tpu_custom_call", output_to_operand_aliasing={{1}: (5, {}), {2}: (6, {})} | custom-call | tf_op jit(solution)/shard_map/attention_1/pallas_call | solution.py:188
  163.9 95.3 %sum_1.1 = bf16[16,64,4096]{2,1,0:T(8,128)(2,1)S(1)} custom-call(bf16[1024,256]{1,0:T(8,128)(2,1)} %bitcast.24, bf16[1024,1024]{1,0:T(8,128)(2,1)} %get-tuple-element.21.refs_1_, bf16[64,4096]{1,0:T(8,128)(2,1)} %get-tuple-element.22.refs_2_, bf16[2,4096]{1,0:T(2,128)(2,1)} %refs_3_.3, bf16[2,256,4096]{2,1,0:T(8,128)(2,1)} %refs_4_.3, ...), custom_call_target="tpu_custom_call" | custom-call | tf_op jit(solution)/shard_map/sum_1/pallas_call | solution.py:430
  259.2 3.4 %copy.31 = bf16[16,64,4096]{2,1,0:T(8,128)(2,1)} copy(bf16[16,64,4096]{2,1,0:T(8,128)(2,1)S(1)} %sum_1.1) | data formatting | bytes 16777216
  (2 shorter events, 0.0 us)
